TPU v7x, 32 devices: a 4x4x1 block of a 4x4x8 slice. The times are simulated.
32 devices in a mesh: rep: 1 (over z), seq: 32 (over y, x, core).
Axes of the slice: x: 4, y: 4, z: 1, core: 2. Of those that a mesh axis runs over, the one named last changes fastest.
The devices are a block of a 4x4x8 slice.
Arguments:
- hidden: bfloat16 [64, 4096], P('rep')
- w_query: bfloat16 [4096, 4096], replicated
- w_key: bfloat16 [4096, 1024], replicated
- w_value: bfloat16 [4096, 1024], replicated
- w_out: bfloat16 [4096, 4096], P('seq')
- k_cache: bfloat16 [64, 2048, 8, 128], P('rep', 'seq')
- v_cache: bfloat16 [64, 2048, 8, 128], P('rep', 'seq')
- positions: int32 [64], P('rep')
Outputs:
- output 1: bfloat16 [64, 4096], P('rep')
- output 2: bfloat16 [64, 2048, 8, 128], P('rep', 'seq')
- output 3: bfloat16 [64, 2048, 8, 128], P('rep', 'seq')
All inputs are finite; a program needn't handle non-finite values.
Results may differ from a plain program's by a relative error of at most 0.00568872.
Values are sent between devices in bfloat16 or wider.
A program may use at most 768 MiB of HBM per device.

v0:
```python
import jax
import jax.numpy as jnp
from jax import lax
from jax.sharding import PartitionSpec as P


def solution(mesh):
    cache_spec = P('rep', 'seq', None, None)
    in_specs = (P('rep', None), P(), P(), P(), P('seq', None), cache_spec, cache_spec, P('rep'))
    out_specs = (P('rep', None), cache_spec, cache_spec)

    def local_step(hidden, w_query, w_key, w_value, w_out, k_cache, v_cache, positions):
        batch_size, local_len, kv_heads, head_dim = k_cache.shape
        num_heads = w_query.shape[1] // head_dim
        group_size = num_heads // kv_heads
        shard_idx = lax.axis_index('seq')
        q_flat = jnp.dot(hidden, w_query, preferred_element_type=jnp.float32).astype(jnp.bfloat16)
        key_new = jnp.dot(hidden, w_key, preferred_element_type=jnp.float32).astype(jnp.bfloat16).reshape(batch_size, kv_heads, head_dim)
        value_new = jnp.dot(hidden, w_value, preferred_element_type=jnp.float32).astype(jnp.bfloat16).reshape(batch_size, kv_heads, head_dim)
        seq_ids = shard_idx * local_len + jnp.arange(local_len)
        at_pos = (seq_ids[None, :] == positions[:, None])[:, :, None, None]
        k_updated = jnp.where(at_pos, key_new[:, None], k_cache)
        v_updated = jnp.where(at_pos, value_new[:, None], v_cache)
        is_valid = (seq_ids[None, :] <= positions[:, None])[:, None, None, :]
        q_heads = q_flat.reshape(batch_size, kv_heads, group_size, head_dim)
        scores = jnp.einsum('bkgd,bskd->bkgs', q_heads, k_updated, preferred_element_type=jnp.float32) * head_dim ** -0.5
        scores = jnp.where(is_valid, scores, -jnp.inf)
        local_max = jnp.max(scores, axis=-1)
        safe_max = jnp.where(jnp.isfinite(local_max), local_max, 0.0)
        weights = jnp.exp(scores - safe_max[..., None])
        local_sum = jnp.sum(weights, axis=-1)
        local_out = jnp.einsum('bkgs,bskd->bkgd', weights.astype(jnp.bfloat16), v_updated, preferred_element_type=jnp.float32)
        global_max = lax.pmax(local_max, 'seq')
        rescale = jnp.exp(local_max - global_max)
        total_sum, total_out = lax.psum((local_sum * rescale, local_out * rescale[..., None]), 'seq')
        combined = (total_out / total_sum[..., None]).astype(jnp.bfloat16).reshape(batch_size, num_heads * head_dim)
        row_count = w_out.shape[0]
        combined_rows = lax.dynamic_slice_in_dim(combined, shard_idx * row_count, row_count, axis=1)
        part_out = jnp.dot(combined_rows, w_out, preferred_element_type=jnp.float32)
        result = lax.psum(part_out, 'seq').astype(jnp.bfloat16)
        return result, k_updated, v_updated

    return jax.shard_map(local_step, mesh=mesh, in_specs=in_specs, out_specs=out_specs, check_vma=False)
```

profile of v0, /device:TPU:97, one launch (start us, length us, event | category | flops | bytes accessed | tf_op | source)
XLA Modules:
  0.0 258.6 jit_solution(2671745320653546293)
XLA Ops:
  7.2 0.0 copy-start
  7.2 0.1 all-reduce.3.cloned.1.call-start
  7.3 0.0 copy-start.1
  7.3 0.0 copy-start.2
  7.3 5.3 %fusion.10 = bf16[8,8,8,128]{3,1,2,0:T(8,128)(2,1)S(1)} fusion(bf16[64,4096]{1,0:T(8,128)(2,1)} %param.8, bf16[4096,1024]{1,0:T(8,128)(2,1)} %param.10), kind=kOutput, calls=%fused_computation.11 | convolution fusion | flops 536936448 | bytes 9043968 | tf_op jit(solution)/shard_map/dot_general | solution.py:18
  12.6 0.7 copy-done.1
  13.3 0.0 copy-done.2
  13.3 1.6 fusion.11
  15.0 0.0 copy-start.4
  15.0 13.6 %convolution_convert_fusion = bf16[64,4096]{1,0:T(8,128)(2,1)S(1)} fusion(bf16[64,4096]{1,0:T(8,128)(2,1)S(1)} %copy-done.2, bf16[4096,4096]{1,0:T(8,128)(2,1)} %param.9), kind=kOutput, calls=%fused_computation.6 | convolution fusion | flops 2147745792 | bytes 34603008 | tf_op jit(solution)/shard_map/dot_general | solution.py:17
  28.6 0.4 reshape.73
  29.0 0.0 copy-done.4
  29.0 0.1 broadcast_compare_fusion.1
  29.1 9.5 %broadcast_select_fusion.1 = (bf16[64,64,8,128]{3,2,1,0:T(8,128)(2,1)S(1)}, bf16[64,64,8,128]{3,2,1,0:T(8,128)(2,1)}) fusion(bf16[64,64,8,128]{3,2,1,0:T(8,128)(2,1)} %param.13, pred[64,64]{1,0:T(8,128)(4,1)S(1)} %get-tuple-element.8, bf16[64,8,128]{2,1,0:T(8,128)(2,1)S(1)} %bitcast.14, bf16[64,64,8,128]{3,2,1,0:T(8,128)(2,1)} %param.14, ...), kind=kLoop, calls=%fused_computation.5 | loop fusion | flops 8388608 | bytes 33820672 | tf_op jit(solution)/shard_map/jit(_where)/select_n | solution.py:22
  38.6 0.0 copy-start.3
  38.6 3.4 %copy-done.3 = bf16[64,64,8,128]{3,2,1,0:T(8,128)(2,1)} copy-done((bf16[64,64,8,128]{3,2,1,0:T(8,128)(2,1)}, bf16[64,64,8,128]{3,2,1,0:T(8,128)(2,1)S(1)}, u32[]{:S(2)}) %copy-start.3) | copy-done | bytes 8388632
  42.0 4.5 %fusion.23 = (f32[64,8,4]{2,1,0:T(8,128)S(1)}, f32[64,8,4,64]{3,2,1,0:T(4,128)S(1)}) fusion(bf16[64,8,4,128]{3,2,1,0:T(4,128)(2,1)S(1)} %reshape.73, bf16[64,64,8,128]{3,2,1,0:T(8,128)(2,1)S(1)} %get-tuple-element.5, pred[64,64]{1,0:T(8,128)(4,1)S(1)} %get-tuple-element.7), kind=kOutput, calls=%fused_computation.28 | convolution fusion | flops 33945600 | bytes 9449472 | tf_op jit(solution)/shard_map/bkgd,bskd->bkgs/dot_general | solution.py:26
  46.5 51.1 %pmax.7 = f32[64,8,4]{2,1,0:T(8,128)S(1)} all-reduce(f32[64,8,4]{2,1,0:T(8,128)S(1)} %get-tuple-element.9), channel_id=1, replica_groups=mesh['rep'=1,'seq'=32] {'seq'}, use_global_device_ids=true, to_apply=%region_1.2 | all-reduce | flops 2048 | bytes 16384 | tf_op jit(solution)/shard_map/pmax | solution.py:33
  97.6 1.3 fusion.15
  98.9 0.1 fusion.22
  99.0 6.8 %fusion.7 = f32[64,8,4,128]{3,2,1,0:T(4,128)} fusion(bf16[64,64,8,128]{3,2,1,0:T(8,128)(2,1)} %get-tuple-element.6, f32[64,8,4,64]{3,2,1,0:T(4,128)S(1)} %get-tuple-element.10, f32[64,8,4]{2,1,0:T(8,128)S(1)} %get-tuple-element.4, f32[64,8,4]{2,1,0:T(8,128)S(1)} %is-finite_select_fusion), kind=kOutput, calls=%fused_computation.8 | convolution fusion | flops 34078720 | bytes 9977856 | tf_op jit(solution)/shard_map/bkgs,bskd->bkgd/dot_general | solution.py:32
  105.8 0.1 all-reduce.3.cloned.1.call-update
  105.8 44.8 %psum.22 = f32[64,8,4]{2,1,0:T(8,128)S(1)} all-reduce(f32[64,8,4]{2,1,0:T(8,128)S(1)} %get-tuple-element.3), channel_id=1, replica_groups=mesh['rep'=1,'seq'=32] {'seq'}, use_global_device_ids=true, to_apply=%region_4.5 | all-reduce | flops 2048 | bytes 16384 | tf_op jit(solution)/shard_map/psum | solution.py:35
  150.6 48.5 %all-reduce.3.cloned.1.call-done = f32[64,8,4,128]{3,2,1,0:T(4,128)} async-done(((f32[64,8,4,128]{3,2,1,0:T(4,128)}), f32[64,8,4,128]{3,2,1,0:T(4,128)}) %all-reduce.3.cloned.1.call-update) | async-done | bytes 1048592 | tf_op jit(solution)/shard_map/psum | solution.py:35
  199.1 1.8 divide_convert_fusion
  200.9 0.4 reshape.74
  201.3 0.0 copy-done
  201.3 0.3 fusion.19
  201.6 50.2 %all-reduce.4 = bf16[64,4096]{1,0:T(8,128)(2,1)} all-reduce(f32[64,4096]{1,0:T(8,128)S(1)} %fusion.19), channel_id=1, replica_groups=mesh['rep'=1,'seq'=32] {'seq'}, use_global_device_ids=true, to_apply=%region_5.6 | all-reduce | flops 262144 | bytes 1572864 | tf_op jit(solution)/shard_map/psum | solution.py:40
  (4 shorter events, 0.1 us)
Async XLA Ops:
  7.2 194.1 %copy-start = (bf16[128,4096]{1,0:T(8,128)(2,1)S(1)}, bf16[128,4096]{1,0:T(8,128)(2,1)}, u32[]{:S(2)}) copy-start(bf16[128,4096]{1,0:T(8,128)(2,1)} %param.12) | copy-start | bytes 3145732
  7.2 191.9 %all-reduce.3.cloned.1.call-start = ((), (), s32[]{:S(2)}) async-start(), calls=%async_computation | async-start | bytes 2097152 | tf_op jit(solution)/shard_map/psum | solution.py:35
  7.3 6.0 %copy-start.1 = (bf16[4096,1024]{1,0:T(8,128)(2,1)S(1)}, bf16[4096,1024]{1,0:T(8,128)(2,1)}, u32[]{:S(2)}) copy-start(bf16[4096,1024]{1,0:T(8,128)(2,1)} %param.11) | copy-start | bytes 25165828
  7.3 6.0 %copy-start.2 = (bf16[64,4096]{1,0:T(8,128)(2,1)S(1)}, bf16[64,4096]{1,0:T(8,128)(2,1)}, u32[]{:S(2)}) copy-start(bf16[64,4096]{1,0:T(8,128)(2,1)} %param.8) | copy-start | bytes 1572868
  15.0 14.0 %copy-start.4 = (s32[64]{0:T(128)S(1)}, s32[64]{0:T(128)}, u32[]{:S(2)}) copy-start(s32[64]{0:T(128)} %param.15) | copy-start | bytes 772
  38.6 3.4 %copy-start.3 = (bf16[64,64,8,128]{3,2,1,0:T(8,128)(2,1)}, bf16[64,64,8,128]{3,2,1,0:T(8,128)(2,1)S(1)}, u32[]{:S(2)}) copy-start(bf16[64,64,8,128]{3,2,1,0:T(8,128)(2,1)S(1)} %get-tuple-element.5) | copy-start | bytes 25165828
Sparse Core Ops, SparseCore 0:
  105.9 93.1 all-reduce.2
where the time goes:
time: 259 us
  blocking collectives  146 us (56%)
  waiting for transfers between devices  48.6 us (19%)
  matrix products  32.1 us (12%)
  between operations  14.2 us (5%)
  other arithmetic  12.7 us (5%)
  local copies, waits for them, and re-layouts  4.94 us (2%)
    pmax x1, blocking collectives, local_step(): global_max = lax.pmax(local_max, 'seq')  51.1 us
    psum x1, blocking collectives, local_step(): result = lax.psum(part_out, 'seq').astype(jnp.bfloat16)  50.2 us
    psum x1, waiting for transfers between devices, local_step(): lax.psum((local_sum * rescale, local_out * rescale[..., None]), 'seq')  48.5 us
    psum x1, blocking collectives, local_step(): lax.psum((local_sum * rescale, local_out * rescale[..., None]), 'seq')  44.8 us
    dot_general x1, matrix products, local_step(): jnp.dot(hidden, w_query, preferred_element_type=jnp.float32)  13.6 us
    select_n x1, other arithmetic, local_step(): k_updated = jnp.where(at_pos, key_new[:, None], k_cache)  9.47 us
    dot_general x1, matrix products, local_step(): jnp.einsum('bkgs,bskd->bkgd', weights.astype(jnp.bfloat16), v_updated, pr...  6.78 us
    dot_general x1, matrix products, local_step(): jnp.dot(hidden, w_key, preferred_element_type=jnp.float32)  5.26 us
  transfers between devices with their start and end apart: 1, of which 1 were waited for; matrix products, arithmetic and copies ran while one was open for 0% of the time, Pallas kernels for 0%

commit v1 on v0

v1 whole, which is shorter than its diff:
```python
import functools
import math

import jax
import jax.numpy as jnp
from jax import lax
from jax.experimental import pallas as pl
from jax.experimental.pallas import tpu as pltpu
from jax.sharding import PartitionSpec as P

F32 = jnp.float32
BF16 = jnp.bfloat16
MESH = pl.DeviceIdType.MESH
VMEM = pltpu.VMEM
DMA = pltpu.SemaphoreType.DMA


def place(n):
    me = lax.axis_index('seq')
    chips = n // 2
    side = math.isqrt(chips)
    chip, core = me // 2, me % 2
    row, col = chip // side, chip % side

    def far(d):
        return min(d[0], side - d[0]) + min(d[1], side - d[1])

    offsets = [(dy, dx) for dy in range(side) for dx in range(side) if dy or dx]
    offsets.sort(key=far, reverse=True)

    def ahead(d):
        return ((row + d[0]) % side) * side + (col + d[1]) % side

    def behind(d):
        return ((row + side - d[0]) % side) * side + (col + side - d[1]) % side

    return me, chip, core, offsets, ahead, behind


def remote(src, dst, send, recv, device):
    return pltpu.make_async_remote_copy(src_ref=src, dst_ref=dst, send_sem=send, recv_sem=recv,
                                        device_id={'seq': device}, device_id_type=MESH)


def greet(core, chip, offsets, ahead):
    barrier = pltpu.get_barrier_semaphore()
    for d in offsets:
        pl.semaphore_signal(barrier, inc=1, device_id={'seq': ahead(d) * 2 + core}, device_id_type=MESH)
    pl.semaphore_signal(barrier, inc=1, device_id={'seq': chip * 2 + 1 - core}, device_id_type=MESH)
    return barrier


def gather_blocks(block, chip, core, offsets, ahead, behind, sems):
    send, recv, fsend, frecv = sems
    partner = chip * 2 + 1 - core
    started = []
    for d in offsets:
        cp = remote(block(core, chip), block(core, chip), send.at[ahead(d)], recv.at[chip], ahead(d) * 2 + core)
        cp.start()
        started.append(cp)
    cp = remote(block(core, chip), block(core, chip), fsend.at[chip], frecv.at[chip], partner)
    cp.start()
    started.append(cp)
    for d in offsets:
        src = behind(d)
        got = block(core, src)
        remote(got, got, send.at[src], recv.at[src], partner).wait_recv()
        cp = remote(got, got, fsend.at[src], frecv.at[src], partner)
        cp.start()
        started.append(cp)
    for src in [chip] + [behind(d) for d in offsets]:
        got = block(1 - core, src)
        remote(got, got, fsend.at[src], frecv.at[src], partner).wait_recv()
    for cp in started:
        cp.wait_send()


def qkv_kernel(n, x_ref, wq_ref, wk_ref, wv_ref, g_ref, wbuf, wsem, send, recv, fsend, frecv):
    me, chip, core, offsets, ahead, behind = place(n)
    barrier = greet(core, chip, offsets, ahead)
    batch, depth = x_ref.shape
    parts = wsem.shape[1]
    step = depth // parts
    wide = wbuf.shape[1] // 2
    kv_heads = wk_ref.shape[1] // wide

    def fetch(w_ref, block, side, j):
        return pltpu.make_async_copy(
            w_ref.at[pl.ds(j * step, step), pl.ds(pl.multiple_of(block * wide, wide), wide)],
            wbuf.at[pl.ds(j * step, step), pl.ds(side * wide, wide)], wsem.at[side, j])

    for j in range(parts):
        fetch(wq_ref, me, 0, j).start()

        @pl.when(chip < kv_heads)
        def _():
            fetch(wk_ref, chip % kv_heads, 1, j).start()

        @pl.when(chip >= kv_heads)
        def _():
            fetch(wv_ref, chip % kv_heads, 1, j).start()

    acc = None
    for j in range(parts):
        fetch(wq_ref, 0, 0, j).wait()
        fetch(wk_ref, 0, 1, j).wait()
        part = jnp.dot(x_ref[:, j * step:(j + 1) * step], wbuf[j * step:(j + 1) * step, :], preferred_element_type=F32)
        acc = part if acc is None else acc + part
    half = batch // 2
    g_ref[core, chip, :batch, :] = acc[:, :wide].astype(BF16)
    kv = jnp.where(core == 0, acc[:half, wide:], acc[half:, wide:])
    g_ref[core, chip, batch:, :] = kv.astype(BF16)
    pl.semaphore_wait(barrier, len(offsets) + 1)
    gather_blocks(lambda c, p: g_ref.at[c, p], chip, core, offsets, ahead, behind, (send, recv, fsend, frecv))


def attend_kernel(pos_ref, g_ref, k_ref, v_ref, ko_ref, vo_ref, o_ref, kbuf, vbuf, qf, knf, vnf, st, sem):
    chunks, per, length, kv_heads, wide = kbuf.shape
    batch = chunks * per
    rows = qf.shape[0] // batch
    chips = rows // 2
    half = batch // 2
    pitch = o_ref.shape[0] // rows
    base = lax.axis_index('seq') * length

    def k_in(i):
        return pltpu.make_async_copy(k_ref.at[pl.ds(i * per, per)], kbuf.at[i], sem.at[0, i])

    def v_in(i):
        return pltpu.make_async_copy(v_ref.at[pl.ds(i * per, per)], vbuf.at[i], sem.at[1, i])

    def k_out(i):
        return pltpu.make_async_copy(kbuf.at[i], ko_ref.at[pl.ds(i * per, per)], sem.at[2, i])

    def v_out(i):
        return pltpu.make_async_copy(vbuf.at[i], vo_ref.at[pl.ds(i * per, per)], sem.at[3, i])

    @pl.loop(0, chunks)
    def _(i):
        k_in(i).start()
        v_in(i).start()

    for r in range(rows):
        qf[pl.ds(r, batch, stride=rows), :] = g_ref[r // chips, r % chips, :batch, :].astype(F32)
    for h in range(kv_heads):
        for c in range(2):
            at = pl.ds(c * half * kv_heads + h, half, stride=kv_heads)
            knf[at, :] = g_ref[c, h, batch:, :].astype(F32)
            vnf[at, :] = g_ref[c, kv_heads + h, batch:, :].astype(F32)
    st[...] = jnp.zeros_like(st)
    cols = length * kv_heads
    col = lax.broadcasted_iota(jnp.int32, (rows, cols), 1)
    row = lax.broadcasted_iota(jnp.int32, (rows, cols), 0)
    ours = (col % kv_heads) == ((row % chips) * 2 * kv_heads // rows)
    place_of = jnp.where(ours, col // kv_heads, 2 ** 30)
    lane = lax.broadcasted_iota(jnp.int32, st.shape, 1)

    @pl.loop(0, chunks)
    def _(i):
        k_in(i).wait()
        v_in(i).wait()
        stats = st[...]
        for j in range(per):
            b = i * per + j
            last = pos_ref[b] - base
            here = (last >= 0) & (last < length)
            at = jnp.clip(last, 0, length - 1)
            new = pl.ds(pl.multiple_of(b * kv_heads, kv_heads), kv_heads)
            kbuf[i, j, at] = jnp.where(here, knf[new, :], kbuf[i, j, at].astype(F32)).astype(BF16)
            vbuf[i, j, at] = jnp.where(here, vnf[new, :], vbuf[i, j, at].astype(F32)).astype(BF16)
            q = qf[pl.ds(pl.multiple_of(b * rows, rows), rows), :].astype(BF16)
            keys = kbuf[i, j].reshape(cols, wide)
            vals = vbuf[i, j].reshape(cols, wide)
            s = lax.dot_general(q, keys, (((1,), (1,)), ((), ())), preferred_element_type=F32) * wide ** -0.5
            s = jnp.where(place_of <= last, s, -jnp.inf)
            m = jnp.max(s, axis=1, keepdims=True)
            w = jnp.exp(s - jnp.where(m == -jnp.inf, 0.0, m))
            total = jnp.sum(w, axis=1, keepdims=True)
            o_ref[pl.ds(b, rows, stride=pitch), :] = jnp.dot(w.astype(BF16), vals, preferred_element_type=F32)
            stats = jnp.where(lane == b, m, stats)
            stats = jnp.where(lane == b + batch, total, stats)
        st[...] = stats
        k_out(i).start()
        v_out(i).start()

    o_ref[pl.ds(batch, rows, stride=pitch), :] = st[...]

    @pl.loop(0, chunks)
    def _(i):
        k_out(i).wait()
        v_out(i).wait()


def merge_kernel(n, o_ref, wo_ref, y_ref, theirs, mine, got, part, ptheirs, pmine, pgot,
                 xs, xr, s1, r1, s2, r2, send, recv, fsend, frecv):
    me, chip, core, offsets, ahead, behind = place(n)
    chips = n // 2
    partner = chip * 2 + 1 - core
    batch, wide = y_ref.shape[0], wo_ref.shape[0]
    pitch = theirs.shape[0] // chips
    barrier = greet(core, chip, offsets, ahead)
    pl.semaphore_wait(barrier, len(offsets) + 1)

    def lanes(x):
        return pltpu.roll(x, batch, 1)

    swap = remote(o_ref.at[pl.ds((1 - core) * chips * pitch, chips * pitch)], theirs, xs.at[0], xr.at[0], partner)
    swap.start()
    swap.wait_recv()
    first = pl.multiple_of(core * chips * pitch, chips * pitch)
    sa = o_ref[pl.ds(first + batch, chips, stride=pitch), :]
    sb = theirs[pl.ds(batch, chips, stride=pitch), :]
    m = jnp.maximum(sa, sb)
    safe = jnp.where(m == -jnp.inf, 0.0, m)
    wa, wb = jnp.exp(sa - safe), jnp.exp(sb - safe)
    total = lanes(sa) * wa + lanes(sb) * wb
    lane = lax.broadcasted_iota(jnp.int32, m.shape, 1)
    mine[pl.ds(batch, chips, stride=pitch), :] = jnp.where(lane < batch, m, lanes(total))
    wt = jnp.concatenate([wa, wb], axis=0).T
    for p in range(chips):
        a = o_ref[pl.ds(first + p * pitch, batch), :] * wt[:batch, p:p + 1]
        b = theirs[p * pitch:p * pitch + batch, :] * wt[:batch, chips + p:chips + p + 1]
        mine[p * pitch:p * pitch + batch, :] = a + b

    def slot(ref, p):
        size = ref.shape[0] // chips
        return ref.at[pl.ds(pl.multiple_of(p * size, size), size)]

    started = []
    for d in offsets:
        to = ahead(d)
        cp = remote(slot(mine, to), slot(got, chip), s1.at[to], r1.at[chip], to * 2 + core)
        cp.start()
        started.append(cp)
    own = pl.ds(pl.multiple_of(chip * pitch, pitch), pitch)
    got[own, :] = mine[own, :]
    for d in offsets:
        src = behind(d)
        remote(slot(got, src), slot(got, src), s1.at[src], r1.at[src], partner).wait_recv()
    s = got[pl.ds(batch, chips, stride=pitch), :]
    w = jnp.exp(s - jnp.max(s, axis=0, keepdims=True))
    w = w / jnp.sum(lanes(s) * w, axis=0, keepdims=True)
    wt = w.T
    out = got[:batch, :] * wt[:batch, 0:1]
    for p in range(1, chips):
        out = out + got[p * pitch:p * pitch + batch, :] * wt[:batch, p:p + 1]
    out = out.astype(BF16)
    for p in range(chips):
        r = jnp.dot(out, wo_ref[:, p * 2 * wide:(p + 1) * 2 * wide], preferred_element_type=F32)
        part[0, p * batch:(p + 1) * batch, :] = r[:, :wide]
        part[1, p * batch:(p + 1) * batch, :] = r[:, wide:]
    swap2 = remote(part.at[1 - core], ptheirs, xs.at[1], xr.at[1], partner)
    swap2.start()
    swap2.wait_recv()
    pmine[...] = part[core] + ptheirs[...]
    for d in offsets:
        to = ahead(d)
        cp = remote(slot(pmine, to), slot(pgot, chip), s2.at[to], r2.at[chip], to * 2 + core)
        cp.start()
        started.append(cp)
    own = pl.ds(pl.multiple_of(chip * batch, batch), batch)
    pgot[own, :] = pmine[own, :]
    for d in offsets:
        src = behind(d)
        remote(slot(pgot, src), slot(pgot, src), s2.at[src], r2.at[src], partner).wait_recv()
    y = pgot[:batch, :]
    for p in range(1, chips):
        y = y + pgot[p * batch:(p + 1) * batch, :]
    y_ref[:, pl.ds(pl.multiple_of(me * wide, wide), wide)] = y.astype(BF16)

    def block(c, p):
        return y_ref.at[:, pl.ds(pl.multiple_of((p * 2 + c) * wide, wide), wide)]

    gather_blocks(block, chip, core, offsets, ahead, behind, (send, recv, fsend, frecv))
    swap.wait_send()
    swap2.wait_send()
    for cp in started:
        cp.wait_send()


def solution(mesh):
    n = mesh.shape['seq']
    chips = n // 2
    cache_spec = P('rep', 'seq', None, None)
    in_specs = (P('rep', None), P(), P(), P(), P('seq', None), cache_spec, cache_spec, P('rep'))
    out_specs = (P('rep', None), cache_spec, cache_spec)
    vmem = pl.BlockSpec(memory_space=pltpu.VMEM)
    smem = pl.BlockSpec(memory_space=pltpu.SMEM)
    hbm = pl.BlockSpec(memory_space=pl.ANY)

    def step(x, wq, wk, wv, wo, k, v, pos):
        batch, depth = x.shape
        length, kv_heads, wide = k.shape[1:]
        heads = wq.shape[1] // wide
        slots = DMA((chips,))
        g = pl.pallas_call(
            functools.partial(qkv_kernel, n),
            out_shape=jax.ShapeDtypeStruct((2, chips, batch + batch // 2, wide), BF16),
            in_specs=[vmem, hbm, hbm, hbm], out_specs=vmem,
            scratch_shapes=[VMEM((depth, 2 * wide), BF16), DMA((2, 4)), slots, slots, slots, slots],
            compiler_params=pltpu.CompilerParams(collective_id=0, has_side_effects=True),
            name='project',
        )(x, wq, wk, wv)
        per = 4
        pitch = batch + 8
        ko, vo, o = pl.pallas_call(
            attend_kernel,
            out_shape=[jax.ShapeDtypeStruct(k.shape, k.dtype), jax.ShapeDtypeStruct(v.shape, v.dtype),
                       jax.ShapeDtypeStruct((heads * pitch, wide), F32)],
            in_specs=[smem, vmem, hbm, hbm], out_specs=[hbm, hbm, vmem],
            scratch_shapes=[VMEM((batch // per, per, length, kv_heads, wide), BF16)] * 2 + [
                VMEM((batch * heads, wide), F32), VMEM((batch * kv_heads, wide), F32),
                VMEM((batch * kv_heads, wide), F32), VMEM((heads, wide), F32), DMA((4, batch // per))],
            name='attend',
        )(pos, g, k, v)
        y = pl.pallas_call(
            functools.partial(merge_kernel, n),
            out_shape=jax.ShapeDtypeStruct((batch, depth), BF16),
            in_specs=[vmem, vmem], out_specs=vmem,
            scratch_shapes=[VMEM((chips * pitch, wide), F32)] * 3 + [VMEM((2, chips * batch, wide), F32)]
            + [VMEM((chips * batch, wide), F32)] * 3 + [DMA((2,))] * 2 + [slots] * 8,
            compiler_params=pltpu.CompilerParams(collective_id=1, has_side_effects=True),
            name='merge',
        )(o, wo)
        return y, ko, vo

    return jax.shard_map(step, mesh=mesh, in_specs=in_specs, out_specs=out_specs, check_vma=False)
```

time: 259 us -> 83.2 us (0.32)
  blocking collectives: 146 us -> 0 us
  Pallas kernels: 0 us -> 80.4 us
  waiting for transfers between devices: 48.6 us -> 0 us
  matrix products: 32.1 us -> 0 us
  between operations: 14.2 us -> 0.65 us
  other arithmetic: 12.7 us -> 0 us
  local copies, waits for them, and re-layouts: 4.94 us -> 1.87 us
    psum x2 -> x0, blocking collectives: 94.9 us -> none  [the longest x1 50.2 us: local_step(): result = lax.psum(part_out, 'seq').astype(jnp.bfloat16)]
    pallas_call x0 -> x3, Pallas kernels: none -> 80.4 us  [the longest x1 37.6 us: step(): pl.pallas_call(functools.partial(merge_kernel, n), out_shape=jax.ShapeDty...]
    pmax x1 -> x0, blocking collectives: 51.1 us -> none  [local_step(): global_max = lax.pmax(local_max, 'seq')]
    psum x1 -> x0, waiting for transfers between devices: 48.5 us -> none  [local_step(): lax.psum((local_sum * rescale, local_out * rescale[..., None]), 'seq')]
    dot_general x6 -> x0, matrix products: 32.1 us -> none  [the longest x1 13.6 us: local_step(): jnp.dot(hidden, w_query, preferred_element_type=jnp.float32)]
    select_n x2 -> x0, other arithmetic: 9.5 us -> none  [the longest x1 9.47 us: local_step(): k_updated = jnp.where(at_pos, key_new[:, None], k_cache)]
  transfers between devices with their start and end apart: 1 -> 0, of which waited for: 1 -> 0; matrix products, arithmetic and copies ran while one was open for 0% -> 0% of each run, Pallas kernels for 0% -> 0%
where the time goes in v1:
time: 83.2 us; the launch traced here: 82.9 us
  Pallas kernels  80.4 us (97%)
  local copies, waits for them, and re-layouts  1.87 us (2%)
    pallas_call x1, Pallas kernels, step(): pl.pallas_call(functools.partial(merge_kernel, n), out_shape=jax.ShapeDty...  37.6 us
    pallas_call x1, Pallas kernels, step(): pl.pallas_call(attend_kernel, out_shape=[jax.ShapeDtypeStruct(k.shape, k....  22.9 us
    pallas_call x1, Pallas kernels, step(): pl.pallas_call(functools.partial(qkv_kernel, n), out_shape=jax.ShapeDtype...  19.9 us
    unnamed x1, local copies, waits for them, and re-layouts  1.87 us

profile of v1, /device:TPU:97, one launch (start us, length us, event | category | flops | bytes accessed | tf_op | source)
XLA Modules:
  0.0 82.9 jit_solution(16274147755847616795)
XLA Ops:
  0.6 19.9 %project.1.g_ref = bf16[2,16,96,128]{3,2,1,0:T(8,128)(2,1)} custom-call(bf16[64,4096]{1,0:T(8,128)(2,1)} %x_ref.1, bf16[4096,4096]{1,0:T(8,128)(2,1)} %wq_ref.1, bf16[4096,1024]{1,0:T(8,128)(2,1)} %wk_ref.1, bf16[4096,1024]{1,0:T(8,128)(2,1)} %wv_ref.1), custom_call_target="tpu_custom_call" | custom-call | tf_op jit(solution)/shard_map/project/pallas_call | solution.py:296
  20.5 22.9 %attend.1 = (bf16[64,64,8,128]{3,2,1,0:T(8,128)(2,1)}, bf16[64,64,8,128]{3,2,1,0:T(8,128)(2,1)}, f32[2304,128]{1,0:T(8,128)}) custom-call(s32[64]{0:T(128)} %pos_ref.1, bf16[2,16,96,128]{3,2,1,0:T(8,128)(2,1)} %project.1.g_ref, bf16[64,64,8,128]{3,2,1,0:T(8,128)(2,1)} %k_ref.1, bf16[64,64,8,128]{3,2,1,0:T(8,128)(2,1)} %v_ref.1), custom_call_target="tpu_custom_call" | custom-call | tf_op jit(solution)/shard_map/attend/pallas_call | solution.py:306
  43.4 37.6 %merge.1 = bf16[64,4096]{1,0:T(8,128)(2,1)} custom-call(f32[2304,128]{1,0:T(8,128)} %get-tuple-element.6.o_ref, bf16[128,4096]{1,0:T(8,128)(2,1)} %wo_ref.1), custom_call_target="tpu_custom_call" | custom-call | tf_op jit(solution)/shard_map/merge/pallas_call | solution.py:316
  81.0 1.9 %copy.12 = bf16[64,4096]{1,0:T(8,128)(2,1)} copy(bf16[64,4096]{1,0:T(8,128)(2,1)} %merge.1) | data formatting | bytes 1048576

commit v2 on v1

v2 whole, which is shorter than its diff:
```python
import functools
import math

import jax
import jax.numpy as jnp
from jax import lax
from jax.experimental import pallas as pl
from jax.experimental.pallas import tpu as pltpu
from jax.sharding import PartitionSpec as P

F32 = jnp.float32
BF16 = jnp.bfloat16
MESH = pl.DeviceIdType.MESH
VMEM = pltpu.VMEM
DMA = pltpu.SemaphoreType.DMA


def place(n):
    me = lax.axis_index('seq')
    chips = n // 2
    side = math.isqrt(chips)
    chip, core = me // 2, me % 2
    row, col = chip // side, chip % side

    def far(d):
        return min(d[0], side - d[0]) + min(d[1], side - d[1])

    offsets = [(dy, dx) for dy in range(side) for dx in range(side) if dy or dx]
    offsets.sort(key=far, reverse=True)

    def ahead(d):
        return ((row + d[0]) % side) * side + (col + d[1]) % side

    def behind(d):
        return ((row + side - d[0]) % side) * side + (col + side - d[1]) % side

    return me, chip, core, offsets, ahead, behind


def remote(src, dst, send, recv, device):
    return pltpu.make_async_remote_copy(src_ref=src, dst_ref=dst, send_sem=send, recv_sem=recv,
                                        device_id={'seq': device}, device_id_type=MESH)


def greet(core, chip, offsets, ahead):
    barrier = pltpu.get_barrier_semaphore()
    for d in offsets:
        pl.semaphore_signal(barrier, inc=1, device_id={'seq': ahead(d) * 2 + core}, device_id_type=MESH)
    pl.semaphore_signal(barrier, inc=1, device_id={'seq': chip * 2 + 1 - core}, device_id_type=MESH)
    return barrier


def gather_blocks(block, chip, core, offsets, ahead, behind, sems, took=None):
    send, recv, fsend, frecv = sems
    partner = chip * 2 + 1 - core
    started = []
    for d in offsets:
        cp = remote(block(core, chip), block(core, chip), send.at[ahead(d)], recv.at[chip], ahead(d) * 2 + core)
        cp.start()
        started.append(cp)
    cp = remote(block(core, chip), block(core, chip), fsend.at[chip], frecv.at[chip], partner)
    cp.start()
    started.append(cp)
    if took is not None:
        took(core, chip)
    for d in offsets:
        src = behind(d)
        got = block(core, src)
        remote(got, got, send.at[src], recv.at[src], partner).wait_recv()
        cp = remote(got, got, fsend.at[src], frecv.at[src], partner)
        cp.start()
        started.append(cp)
        if took is not None:
            took(core, src)
    for src in [chip] + [behind(d) for d in offsets]:
        got = block(1 - core, src)
        remote(got, got, fsend.at[src], frecv.at[src], partner).wait_recv()
        if took is not None:
            took(1 - core, src)
    return started


def decode_kernel(n, pos_ref, x_ref, wq_ref, wk_ref, wv_ref, wo_ref, k_ref, v_ref, y_ref, kn_ref, vn_ref,
                  wbuf, g_ref, kbuf, vbuf, qf, kvf, st, o_ref, theirs, mine, got, part, ptheirs, pmine, pgot,
                  wsem, ksem, asend, arecv, afsend, afrecv, xs, xr, s1, r1, s2, r2, send, recv, fsend, frecv):
    me, chip, core, offsets, ahead, behind = place(n)
    chips = n // 2
    partner = chip * 2 + 1 - core
    barrier = greet(core, chip, offsets, ahead)
    batch, depth = x_ref.shape
    wide = wbuf.shape[1] // 2
    groups, per, length, kv_heads, _ = kbuf.shape
    rows = qf.shape[0] // batch
    half = batch // 2
    pitch = theirs.shape[0] // chips
    base = me * length

    parts = wsem.shape[1]
    step = depth // parts

    def fetch(w_ref, block, side, j):
        return pltpu.make_async_copy(
            w_ref.at[pl.ds(j * step, step), pl.ds(pl.multiple_of(block * wide, wide), wide)],
            wbuf.at[pl.ds(j * step, step), pl.ds(side * wide, wide)], wsem.at[side, j])

    for j in range(parts):
        fetch(wq_ref, me, 0, j).start()

        @pl.when(chip < kv_heads)
        def _():
            fetch(wk_ref, chip % kv_heads, 1, j).start()

        @pl.when(chip >= kv_heads)
        def _():
            fetch(wv_ref, chip % kv_heads, 1, j).start()

    def k_in(i):
        return pltpu.make_async_copy(k_ref.at[:, i], kbuf.at[i], ksem.at[0, i])

    def v_in(i):
        return pltpu.make_async_copy(v_ref.at[:, i], vbuf.at[i], ksem.at[1, i])

    @pl.loop(0, groups)
    def _(i):
        k_in(i).start()
        v_in(i).start()

    st[...] = jnp.zeros_like(st)
    acc = None
    for j in range(parts):
        fetch(wq_ref, 0, 0, j).wait()
        fetch(wk_ref, 0, 1, j).wait()
        one = jnp.dot(x_ref[:, j * step:(j + 1) * step], wbuf[j * step:(j + 1) * step, :], preferred_element_type=F32)
        acc = one if acc is None else acc + one
    g_ref[core, chip, :batch, :] = acc[:, :wide].astype(BF16)
    kv = jnp.where(core == 0, acc[:half, wide:], acc[half:, wide:])
    g_ref[core, chip, batch:, :] = kv.astype(BF16)
    pl.semaphore_wait(barrier, len(offsets) + 1)

    def took(c, p):
        r = c * chips + p
        for j in range(per):
            qf[pl.ds(j * rows + r, groups, stride=per * rows), :] = g_ref[c, p, j * groups:(j + 1) * groups, :].astype(F32)
        at = (p // kv_heads) * batch * kv_heads + c * half * kv_heads + p % kv_heads
        kvf[pl.ds(at, half, stride=kv_heads), :] = g_ref[c, p, batch:, :].astype(F32)

    started = gather_blocks(lambda c, p: g_ref.at[c, p], chip, core, offsets, ahead, behind,
                            (asend, arecv, afsend, afrecv), took)

    cols = length * kv_heads
    lane = lax.broadcasted_iota(jnp.int32, (kv_heads, wide), 1)
    sub = lax.broadcasted_iota(jnp.int32, (kv_heads, wide), 0)
    ours = sub == ((lane % chips) * 2 * kv_heads // rows)
    quarter = lane // rows
    wlane = lax.broadcasted_iota(jnp.int32, (wide, wide), 1) // rows

    @pl.loop(0, groups)
    def _(i):
        k_in(i).wait()
        v_in(i).wait()
        last = jnp.zeros((kv_heads, wide), jnp.int32)
        for j in range(per):
            b = j * groups + i
            end = pos_ref[b] - base
            last = jnp.where(quarter == j, end, last)
            here = (end >= 0) & (end < length)
            at = jnp.clip(end, 0, length - 1)
            new = kvf[pl.ds(pl.multiple_of(b * kv_heads, kv_heads), kv_heads), :].astype(BF16)
            kn_ref[b] = new
            kbuf[i, j] = jnp.where(patch_rows(length, kv_heads, wide, at, here), new[None], kbuf[i, j])
            new = kvf[pl.ds(pl.multiple_of((batch + b) * kv_heads, kv_heads), kv_heads), :].astype(BF16)
            vn_ref[b] = new
            vbuf[i, j] = jnp.where(patch_rows(length, kv_heads, wide, at, here), new[None], vbuf[i, j])
        limit = jnp.where(ours, last, -1)
        qt = qf[pl.ds(pl.multiple_of(i * per * rows, per * rows), per * rows), :].T.astype(BF16)
        keys = jnp.concatenate([kbuf[i, j].reshape(cols, wide) for j in range(per)], axis=1)
        query = jnp.concatenate([jnp.where(wlane == j, qt, 0) for j in range(per)], axis=0)
        s = jnp.dot(keys, query, preferred_element_type=F32).reshape(length, kv_heads, wide) * wide ** -0.5
        t = lax.broadcasted_iota(jnp.int32, (length, kv_heads, wide), 0)
        s = jnp.where(t <= limit[None], s, -jnp.inf)
        m = jnp.max(jnp.max(s, axis=0), axis=0, keepdims=True)
        w = jnp.exp(s - jnp.where(m == -jnp.inf, 0.0, m)[None])
        st[pl.ds(i, 1), :] = m
        st[pl.ds(groups + i, 1), :] = jnp.sum(jnp.sum(w, axis=0), axis=0, keepdims=True)
        wt = w.reshape(cols, wide).T.astype(BF16)
        for j in range(per):
            o_ref[pl.ds(j * groups + i, rows, stride=pitch), :] = jnp.dot(
                wt[j * rows:(j + 1) * rows, :], vbuf[i, j].reshape(cols, wide), preferred_element_type=F32)

    zt = st[...].T
    slane = lax.broadcasted_iota(jnp.int32, (rows, wide), 1) // groups
    stats = jnp.zeros((rows, wide), F32)
    for j in range(per):
        z = zt[j * rows:(j + 1) * rows, :]
        stats = jnp.where(slane == j, pltpu.roll(z, j * groups, 1) if j else z, stats)
        stats = jnp.where(slane == per + j, pltpu.roll(z, batch + j * groups - groups, 1), stats)
    o_ref[pl.ds(batch, rows, stride=pitch), :] = stats

    def lanes(x):
        return pltpu.roll(x, batch, 1)

    swap = remote(o_ref.at[pl.ds((1 - core) * chips * pitch, chips * pitch)], theirs, xs.at[0], xr.at[0], partner)
    swap.start()
    swap.wait_recv()
    first = pl.multiple_of(core * chips * pitch, chips * pitch)
    sa = o_ref[pl.ds(first + batch, chips, stride=pitch), :]
    sb = theirs[pl.ds(batch, chips, stride=pitch), :]
    m = jnp.maximum(sa, sb)
    safe = jnp.where(m == -jnp.inf, 0.0, m)
    wa, wb = jnp.exp(sa - safe), jnp.exp(sb - safe)
    total = lanes(sa) * wa + lanes(sb) * wb
    lane = lax.broadcasted_iota(jnp.int32, m.shape, 1)
    mine[pl.ds(batch, chips, stride=pitch), :] = jnp.where(lane < batch, m, lanes(total))
    wt = jnp.concatenate([wa, wb], axis=0).T
    for p in range(chips):
        a = o_ref[pl.ds(first + p * pitch, batch), :] * wt[:batch, p:p + 1]
        b = theirs[p * pitch:p * pitch + batch, :] * wt[:batch, chips + p:chips + p + 1]
        mine[p * pitch:p * pitch + batch, :] = a + b

    def slot(ref, p):
        size = ref.shape[0] // chips
        return ref.at[pl.ds(pl.multiple_of(p * size, size), size)]

    for d in offsets:
        to = ahead(d)
        cp = remote(slot(mine, to), slot(got, chip), s1.at[to], r1.at[chip], to * 2 + core)
        cp.start()
        started.append(cp)
    own = pl.ds(pl.multiple_of(chip * pitch, pitch), pitch)
    got[own, :] = mine[own, :]
    for d in offsets:
        src = behind(d)
        remote(slot(got, src), slot(got, src), s1.at[src], r1.at[src], partner).wait_recv()
    s = got[pl.ds(batch, chips, stride=pitch), :]
    w = jnp.exp(s - jnp.max(s, axis=0, keepdims=True))
    w = w / jnp.sum(lanes(s) * w, axis=0, keepdims=True)
    wt = w.T
    out = got[:batch, :] * wt[:batch, 0:1]
    for p in range(1, chips):
        out = out + got[p * pitch:p * pitch + batch, :] * wt[:batch, p:p + 1]
    out = out.astype(BF16)
    for p in range(chips):
        r = jnp.dot(out, wo_ref[:, p * 2 * wide:(p + 1) * 2 * wide], preferred_element_type=F32)
        part[0, p * batch:(p + 1) * batch, :] = r[:, :wide]
        part[1, p * batch:(p + 1) * batch, :] = r[:, wide:]
    swap2 = remote(part.at[1 - core], ptheirs, xs.at[1], xr.at[1], partner)
    swap2.start()
    swap2.wait_recv()
    pmine[...] = part[core] + ptheirs[...]
    for d in offsets:
        to = ahead(d)
        cp = remote(slot(pmine, to), slot(pgot, chip), s2.at[to], r2.at[chip], to * 2 + core)
        cp.start()
        started.append(cp)
    own = pl.ds(pl.multiple_of(chip * batch, batch), batch)
    pgot[own, :] = pmine[own, :]
    for d in offsets:
        src = behind(d)
        remote(slot(pgot, src), slot(pgot, src), s2.at[src], r2.at[src], partner).wait_recv()
    y = pgot[:batch, :]
    for p in range(1, chips):
        y = y + pgot[p * batch:(p + 1) * batch, :]
    y_ref[:, pl.ds(pl.multiple_of(me * wide, wide), wide)] = y.astype(BF16)

    def block(c, p):
        return y_ref.at[:, pl.ds(pl.multiple_of((p * 2 + c) * wide, wide), wide)]

    started += gather_blocks(block, chip, core, offsets, ahead, behind, (send, recv, fsend, frecv))
    swap.wait_send()
    swap2.wait_send()
    for cp in started:
        cp.wait_send()


def store_kernel(pos_ref, k_ref, v_ref, kn_ref, vn_ref, y_ref, ko_ref, vo_ref, yo_ref, sem, rsem, ysem):
    batch, length = k_ref.shape[:2]
    chunks = sem.shape[1]
    per = batch // chunks
    base = lax.axis_index('seq') * length

    def whole(src, dst, a, i):
        return pltpu.make_async_copy(src.at[pl.ds(i * per, per)], dst.at[pl.ds(i * per, per)], sem.at[a, i])

    def row(src, dst, a, b):
        at = jnp.clip(pos_ref[b] - base, 0, length - 1)
        return pltpu.make_async_copy(src.at[b], dst.at[b, at], rsem.at[a, b])

    def here(b):
        end = pos_ref[b] - base
        return (end >= 0) & (end < length)

    @pl.loop(0, chunks)
    def _(i):
        whole(k_ref, ko_ref, 0, i).start()
        whole(v_ref, vo_ref, 1, i).start()

    y = pltpu.make_async_copy(y_ref, yo_ref, ysem)
    y.start()

    @pl.loop(0, chunks)
    def _(i):
        whole(k_ref, ko_ref, 0, i).wait()
        whole(v_ref, vo_ref, 1, i).wait()
        for j in range(per):
            b = i * per + j

            @pl.when(here(b))
            def _():
                row(kn_ref, ko_ref, 0, b).start()
                row(vn_ref, vo_ref, 1, b).start()

    y.wait()

    @pl.loop(0, batch)
    def _(b):
        @pl.when(here(b))
        def _():
            row(kn_ref, ko_ref, 0, b).wait()
            row(vn_ref, vo_ref, 1, b).wait()


def patch_rows(length, kv_heads, wide, at, here):
    t = lax.broadcasted_iota(jnp.int32, (length, kv_heads, wide), 0)
    return (t == at) & here


def solution(mesh):
    n = mesh.shape['seq']
    chips = n // 2
    cache_spec = P('rep', 'seq', None, None)
    in_specs = (P('rep', None), P(), P(), P(), P('seq', None), cache_spec, cache_spec, P('rep'))
    out_specs = (P('rep', None), cache_spec, cache_spec)
    vmem = pl.BlockSpec(memory_space=pltpu.VMEM)
    smem = pl.BlockSpec(memory_space=pltpu.SMEM)
    hbm = pl.BlockSpec(memory_space=pltpu.HBM)
    anywhere = pl.BlockSpec(memory_space=pl.ANY)

    def step(x, wq, wk, wv, wo, k, v, pos):
        batch, depth = x.shape
        length, kv_heads, wide = k.shape[1:]
        heads = wq.shape[1] // wide
        slots = DMA((chips,))
        per = wide // heads
        groups = batch // per
        pitch = batch + 8
        split = (per, groups, length, kv_heads, wide)
        cache = VMEM((groups, per, length, kv_heads, wide), BF16)
        new = jax.ShapeDtypeStruct((batch, kv_heads, wide), BF16)
        y, kn, vn = pl.pallas_call(
            functools.partial(decode_kernel, n),
            out_shape=[jax.ShapeDtypeStruct((batch, depth), BF16), new, new],
            in_specs=[smem, vmem, hbm, hbm, hbm, vmem, hbm, hbm], out_specs=[vmem] * 3,
            scratch_shapes=[
                VMEM((depth, 2 * wide), BF16), VMEM((2, chips, batch + batch // 2, wide), BF16), cache, cache,
                VMEM((batch * heads, wide), F32), VMEM((2 * batch * kv_heads, wide), F32), VMEM((wide, wide), F32),
                VMEM((heads * pitch, wide), F32)]
            + [VMEM((chips * pitch, wide), F32)] * 3 + [VMEM((2, chips * batch, wide), F32)]
            + [VMEM((chips * batch, wide), F32)] * 3 + [DMA((2, 4)), DMA((2, groups))] + [slots] * 4
            + [DMA((2,))] * 2 + [slots] * 8,
            compiler_params=pltpu.CompilerParams(collective_id=0, has_side_effects=True, vmem_limit_bytes=44 << 20),
            cost_estimate=pl.CostEstimate(flops=10 ** 10, bytes_accessed=32 << 20, transcendentals=0),
            name='decode',
        )(pos, x, wq, wk, wv, wo, k.reshape(split), v.reshape(split))
        chunks = 16
        ko, vo, y = pl.pallas_call(
            store_kernel,
            out_shape=[jax.ShapeDtypeStruct(k.shape, k.dtype), jax.ShapeDtypeStruct(v.shape, v.dtype),
                       jax.ShapeDtypeStruct((batch, depth), BF16)],
            in_specs=[smem, anywhere, anywhere, vmem, vmem, vmem], out_specs=[hbm, hbm, hbm],
            scratch_shapes=[DMA((2, chunks)), DMA((2, batch)), DMA],
            compiler_params=pltpu.CompilerParams(vmem_limit_bytes=4 << 20),
            cost_estimate=pl.CostEstimate(flops=10 ** 8, bytes_accessed=32 << 20, transcendentals=0),
            name='store',
        )(pos, k, v, kn, vn, y)
        return y, ko, vo

    return jax.shard_map(step, mesh=mesh, in_specs=in_specs, out_specs=out_specs, check_vma=False)
```

time: 83.2 us -> 75.7 us (0.910)
  Pallas kernels: 80.4 us -> 71.9 us
  local copies, waits for them, and re-layouts: 1.87 us -> 2.92 us
    pallas_call x3 -> x2, Pallas kernels: 80.4 us -> 71.9 us  [the longest x1 64 us: step(): pl.pallas_call(functools.partial(decode_kernel, n), out_shape=[jax.ShapeD...]
    unnamed x1 -> x10, local copies, waits for them, and re-layouts: 1.87 us -> 2.92 us
where the time goes in v2:
time: 75.7 us; the launch traced here: 75.5 us
  Pallas kernels  71.9 us (95%)
  local copies, waits for them, and re-layouts  2.92 us (4%)
    pallas_call x1, Pallas kernels, step(): pl.pallas_call(functools.partial(decode_kernel, n), out_shape=[jax.ShapeD...  64 us
    pallas_call x1, Pallas kernels, step(): pl.pallas_call(store_kernel, out_shape=[jax.ShapeDtypeStruct(k.shape, k.d...  7.94 us
    unnamed x10, local copies, waits for them, and re-layouts  2.92 us

profile of v2, /device:TPU:97, one launch (start us, length us, event | category | flops | bytes accessed | tf_op | source)
XLA Modules:
  0.0 75.5 jit_solution(3784564307562509042)
XLA Ops:
  0.6 0.0 copy-start.2
  0.6 1.2 %copy-done.2 = bf16[128,4096]{1,0:T(8,128)(2,1)S(1)} copy-done((bf16[128,4096]{1,0:T(8,128)(2,1)S(1)}, bf16[128,4096]{1,0:T(8,128)(2,1)}, u32[]{:S(2)}) %copy-start.2) | copy-done | bytes 1048600
  1.9 0.0 copy-start.3
  1.9 1.0 %copy-done.3 = bf16[64,4096]{1,0:T(8,128)(2,1)S(1)} copy-done((bf16[64,4096]{1,0:T(8,128)(2,1)S(1)}, bf16[64,4096]{1,0:T(8,128)(2,1)}, u32[]{:S(2)}) %copy-start.3) | copy-done | bytes 524312
  2.9 0.0 copy-start.4
  2.9 0.7 copy-done.4
  3.6 0.0 copy-start
  3.6 0.0 copy-start.1
  3.6 64.0 %decode.1 = (bf16[64,4096]{1,0:T(8,128)(2,1)S(1)}, bf16[64,8,128]{2,1,0:T(8,128)(2,1)S(1)}, bf16[64,8,128]{2,1,0:T(8,128)(2,1)S(1)}) custom-call(s32[64]{0:T(128)S(1)} %copy-done.4, bf16[64,4096]{1,0:T(8,128)(2,1)S(1)} %copy-done.3, bf16[4096,4096]{1,0:T(8,128)(2,1)} %wq_ref.1, bf16[4096,1024]{1,0:T(8,128)(2,1)} %wk_ref.1, bf16[4096,1024]{1,0:T(8,128)(2,1)} %wv_ref.1, ...), custom_call_target="tpu_custom_call" | custom-call | flops 10000000000 | bytes 33554432 | tf_op jit(solution)/shard_map/decode/pallas_call | solution.py:349
  67.5 0.0 copy-done
  67.6 0.0 copy-done.1
  67.6 7.9 %store.1 = (bf16[64,64,8,128]{3,2,1,0:T(8,128)(2,1)}, bf16[64,64,8,128]{3,2,1,0:T(8,128)(2,1)}, bf16[64,4096]{1,0:T(8,128)(2,1)}) custom-call(s32[64]{0:T(128)S(1)} %copy-done.4, bf16[64,64,8,128]{3,2,1,0:T(8,128)(2,1)S(1)} %copy-done, bf16[64,64,8,128]{3,2,1,0:T(8,128)(2,1)S(1)} %copy-done.1, bf16[64,8,128]{2,1,0:T(8,128)(2,1)S(1)} %get-tuple-element.9.kn_ref, ...), custom_call_target="tpu_custom_call" | custom-call | flops 100000000 | bytes 33554432 | tf_op jit(solution)/shard_map/store/pallas_call | solution.py:365
Async XLA Ops:
  0.6 1.2 %copy-start.2 = (bf16[128,4096]{1,0:T(8,128)(2,1)S(1)}, bf16[128,4096]{1,0:T(8,128)(2,1)}, u32[]{:S(2)}) copy-start(bf16[128,4096]{1,0:T(8,128)(2,1)} %wo_ref.1) | copy-start | bytes 3145732
  1.9 1.0 %copy-start.3 = (bf16[64,4096]{1,0:T(8,128)(2,1)S(1)}, bf16[64,4096]{1,0:T(8,128)(2,1)}, u32[]{:S(2)}) copy-start(bf16[64,4096]{1,0:T(8,128)(2,1)} %x_ref.1) | copy-start | bytes 1572868
  2.9 0.7 copy-start.4
  3.6 64.0 %copy-start = (bf16[64,64,8,128]{3,2,1,0:T(8,128)(2,1)S(1)}, bf16[64,64,8,128]{3,2,1,0:T(8,128)(2,1)}, u32[]{:S(2)}) copy-start(bf16[64,64,8,128]{3,2,1,0:T(8,128)(2,1)} %k_ref.1) | copy-start | bytes 25165828
  3.6 64.0 %copy-start.1 = (bf16[64,64,8,128]{3,2,1,0:T(8,128)(2,1)S(1)}, bf16[64,64,8,128]{3,2,1,0:T(8,128)(2,1)}, u32[]{:S(2)}) copy-start(bf16[64,64,8,128]{3,2,1,0:T(8,128)(2,1)} %v_ref.1) | copy-start | bytes 25165828

commit v3 on v2

v3 whole, which is shorter than its diff:
```python
import functools
import math

import jax
import jax.numpy as jnp
from jax import lax
from jax.experimental import pallas as pl
from jax.experimental.pallas import tpu as pltpu
from jax.sharding import PartitionSpec as P

F32 = jnp.float32
BF16 = jnp.bfloat16
MESH = pl.DeviceIdType.MESH
VMEM = pltpu.VMEM
DMA = pltpu.SemaphoreType.DMA


def place(n):
    me = lax.axis_index('seq')
    chips = n // 2
    side = math.isqrt(chips)
    chip, core = me // 2, me % 2
    row, col = chip // side, chip % side

    def far(d):
        return min(d[0], side - d[0]) + min(d[1], side - d[1])

    offsets = [(dy, dx) for dy in range(side) for dx in range(side) if dy or dx]
    offsets.sort(key=far, reverse=True)

    def ahead(d):
        return ((row + d[0]) % side) * side + (col + d[1]) % side

    def behind(d):
        return ((row + side - d[0]) % side) * side + (col + side - d[1]) % side

    return me, chip, core, offsets, ahead, behind


def remote(src, dst, send, recv, device):
    return pltpu.make_async_remote_copy(src_ref=src, dst_ref=dst, send_sem=send, recv_sem=recv,
                                        device_id={'seq': device}, device_id_type=MESH)


def greet(core, chip, offsets, ahead):
    barrier = pltpu.get_barrier_semaphore()
    for d in offsets:
        pl.semaphore_signal(barrier, inc=1, device_id={'seq': ahead(d) * 2 + core}, device_id_type=MESH)
    pl.semaphore_signal(barrier, inc=1, device_id={'seq': chip * 2 + 1 - core}, device_id_type=MESH)
    return barrier


def gather_blocks(block, chip, core, offsets, ahead, behind, sems, took=None):
    send, recv, fsend, frecv = sems
    partner = chip * 2 + 1 - core
    started = []
    for d in offsets:
        cp = remote(block(core, chip), block(core, chip), send.at[ahead(d)], recv.at[chip], ahead(d) * 2 + core)
        cp.start()
        started.append(cp)
    cp = remote(block(core, chip), block(core, chip), fsend.at[chip], frecv.at[chip], partner)
    cp.start()
    started.append(cp)
    if took is not None:
        took(core, chip)
    for d in offsets:
        src = behind(d)
        got = block(core, src)
        remote(got, got, send.at[src], recv.at[src], partner).wait_recv()
        cp = remote(got, got, fsend.at[src], frecv.at[src], partner)
        cp.start()
        started.append(cp)
        if took is not None:
            took(core, src)
    for src in [chip] + [behind(d) for d in offsets]:
        got = block(1 - core, src)
        remote(got, got, fsend.at[src], frecv.at[src], partner).wait_recv()
        if took is not None:
            took(1 - core, src)
    return started


def decode_kernel(n, pos_ref, x_ref, wq_ref, wk_ref, wv_ref, wo_ref, k_ref, v_ref, y_ref, kn_ref, vn_ref,
                  pos, x, wo, wbuf, g_ref, kbuf, vbuf, qf, kvf, o_ref, theirs, mine, got, part, ptheirs, pmine, pgot,
                  isem, wsem, ksem, asend, arecv, afsend, afrecv, xs, xr, s1, r1, s2, r2, send, recv, fsend, frecv):
    me, chip, core, offsets, ahead, behind = place(n)
    chips = n // 2
    partner = chip * 2 + 1 - core
    barrier = greet(core, chip, offsets, ahead)
    batch, depth = x.shape
    wide = wbuf.shape[1] // 2
    groups, per, length, kv_heads, _ = kbuf.shape
    rows = qf.shape[0] // batch
    half = batch // 2
    halves = theirs.shape[0]
    pitch = theirs.shape[1] // chips
    share = batch // halves
    base = me * length

    parts = wsem.shape[1]
    step = depth // parts

    def fetch(w_ref, block, side, j):
        return pltpu.make_async_copy(
            w_ref.at[pl.ds(j * step, step), pl.ds(pl.multiple_of(block * wide, wide), wide)],
            wbuf.at[pl.ds(j * step, step), pl.ds(side * wide, wide)], wsem.at[side, j])

    get_x = pltpu.make_async_copy(x_ref, x, isem.at[0])
    get_x.start()
    for j in range(parts):
        fetch(wq_ref, me, 0, j).start()

        @pl.when(chip < kv_heads)
        def _():
            fetch(wk_ref, chip % kv_heads, 1, j).start()

        @pl.when(chip >= kv_heads)
        def _():
            fetch(wv_ref, chip % kv_heads, 1, j).start()

    get_pos = pltpu.make_async_copy(pos_ref, pos, isem.at[1])
    get_pos.start()

    def k_in(i):
        return pltpu.make_async_copy(k_ref.at[pl.ds(i * per, per)], kbuf.at[i], ksem.at[0, i])

    def v_in(i):
        return pltpu.make_async_copy(v_ref.at[pl.ds(i * per, per)], vbuf.at[i], ksem.at[1, i])

    get_x.wait()
    acc = None
    for j in range(parts):
        fetch(wq_ref, 0, 0, j).wait()
        fetch(wk_ref, 0, 1, j).wait()
        one = jnp.dot(x[:, j * step:(j + 1) * step], wbuf[j * step:(j + 1) * step, :], preferred_element_type=F32)
        acc = one if acc is None else acc + one
    g_ref[core, chip, :batch, :] = acc[:, :wide].astype(BF16)
    kv = jnp.where(core == 0, acc[:half, wide:], acc[half:, wide:])
    g_ref[core, chip, batch:, :] = kv.astype(BF16)

    @pl.loop(0, groups)
    def _(i):
        k_in(i).start()
        v_in(i).start()

    get_wo = pltpu.make_async_copy(wo_ref, wo, isem.at[2])
    get_wo.start()
    pl.semaphore_wait(barrier, len(offsets) + 1)

    def took(c, p):
        qf[pl.ds(c * chips + p, batch, stride=rows), :] = g_ref[c, p, :batch, :].astype(F32)
        at = (p // kv_heads) * batch * kv_heads + c * half * kv_heads + p % kv_heads
        kvf[pl.ds(at, half, stride=kv_heads), :] = g_ref[c, p, batch:, :].astype(F32)

    started = gather_blocks(lambda c, p: g_ref.at[c, p], chip, core, offsets, ahead, behind,
                            (asend, arecv, afsend, afrecv), took)
    get_pos.wait()

    cols = length * kv_heads
    lanes = per * rows
    lane = lax.broadcasted_iota(jnp.int32, (kv_heads, lanes), 1)
    sub = lax.broadcasted_iota(jnp.int32, (kv_heads, lanes), 0)
    ours = sub == ((lane % chips) * 2 * kv_heads // rows)
    member = lane // rows
    qlane = lax.broadcasted_iota(jnp.int32, (wide, lanes), 1) // rows
    slane = lax.broadcasted_iota(jnp.int32, (rows, wide), 1)

    def attend(i, stats):
        k_in(i).wait()
        v_in(i).wait()
        end = jnp.zeros((kv_heads, lanes), jnp.int32)
        fresh = []
        for j in range(per):
            b = i * per + j
            end = jnp.where(member == j, pos[b] - base, end)
            kn = kvf[pl.ds(pl.multiple_of(b * kv_heads, kv_heads), kv_heads), :].astype(BF16)
            vn = kvf[pl.ds(pl.multiple_of((batch + b) * kv_heads, kv_heads), kv_heads), :].astype(BF16)
            kn_ref[b] = kn
            vn_ref[b] = vn
            fresh.append((kn, vn))
        qt = qf[pl.ds(pl.multiple_of(i * lanes, lanes), lanes), :].T.astype(BF16)
        query = jnp.concatenate([jnp.where(qlane == j, qt, 0) for j in range(per)], axis=0)
        keys = jnp.concatenate([kbuf[i, j].reshape(cols, wide) for j in range(per)], axis=1)
        scale = wide ** -0.5
        s = jnp.dot(keys, query, preferred_element_type=F32).reshape(length, kv_heads, lanes) * scale
        newest = jnp.dot(jnp.concatenate([f[0] for f in fresh], axis=1), query, preferred_element_type=F32) * scale
        t = lax.broadcasted_iota(jnp.int32, (length, kv_heads, lanes), 0)
        s = jnp.where(t < jnp.where(ours, end, 0)[None], s, -jnp.inf)
        newest = jnp.where(ours & (end >= 0) & (end < length), newest, -jnp.inf)
        m = jnp.max(jnp.maximum(jnp.max(s, axis=0), newest), axis=0, keepdims=True)
        safe = jnp.where(m == -jnp.inf, 0.0, m)
        w = jnp.exp(s - safe[None])
        nw = jnp.exp(newest - safe)
        total = jnp.sum(jnp.sum(w, axis=0) + nw, axis=0, keepdims=True)
        wt = w.reshape(cols, lanes).T.astype(BF16)
        extra = jnp.concatenate([nw, m, total, jnp.zeros((kv_heads - 2, lanes), F32)], axis=0).T
        at = (i // (groups // halves)) * rows * pitch + (i % (groups // halves)) * per
        for j in range(0, per, 2):
            both = slice(j * rows, (j + 2) * rows)
            vals = jnp.concatenate([vbuf[i, j].reshape(cols, wide), vbuf[i, j + 1].reshape(cols, wide)], axis=1)
            news = jnp.concatenate([fresh[j][1], fresh[j + 1][1]], axis=1)
            o = jnp.dot(wt[both], vals, preferred_element_type=F32)
            o = o + jnp.dot(extra[both, :kv_heads].astype(BF16), news, preferred_element_type=F32)
            o_ref[pl.ds(at + j, rows, stride=pitch), :] = o[:rows, :wide]
            o_ref[pl.ds(at + j + 1, rows, stride=pitch), :] = o[rows:, wide:]
        for j in range(per):
            z = extra[j * rows:(j + 1) * rows, :]
            stats = jnp.where(slane == i * per + j, z[:, kv_heads:kv_heads + 1], stats)
            stats = jnp.where(slane == batch + i * per + j, z[:, kv_heads + 1:kv_heads + 2], stats)
        return stats

    def other(v):
        return pltpu.roll(v, batch, 1)

    def swap(t):
        return remote(o_ref.at[pl.ds(pl.multiple_of((t * 2 + 1 - core) * chips * pitch, chips * pitch), chips * pitch)],
                      theirs.at[t], xs.at[t], xr.at[t], partner)

    mlane = lax.broadcasted_iota(jnp.int32, (chips, wide), 1)

    def merge_pair(t):
        swap(t).wait_recv()
        first = pl.multiple_of((t * 2 + core) * chips * pitch, chips * pitch)
        sa = o_ref[pl.ds(first + share, chips, stride=pitch), :]
        sb = theirs[t, pl.ds(share, chips, stride=pitch), :]
        m = jnp.maximum(sa, sb)
        safe = jnp.where(m == -jnp.inf, 0.0, m)
        wa, wb = jnp.exp(sa - safe), jnp.exp(sb - safe)
        total = other(sa) * wa + other(sb) * wb
        mine[t, pl.ds(share, chips, stride=pitch), :] = jnp.where(mlane < batch, m, other(total))
        wt = jnp.concatenate([wa, wb], axis=0).T
        mid = slice(t * share, (t + 1) * share)
        for p in range(chips):
            a = o_ref[pl.ds(first + p * pitch, share), :] * wt[mid, p:p + 1]
            b = theirs[t, p * pitch:p * pitch + share, :] * wt[mid, chips + p:chips + p + 1]
            mine[t, p * pitch:p * pitch + share, :] = a + b
        for d in offsets:
            to = ahead(d)
            cp = remote(slot(mine.at[t], to), slot(got.at[t], chip), s1.at[t, to], r1.at[t, chip], to * 2 + core)
            cp.start()
            started.append(cp)
        own = pl.ds(pl.multiple_of(chip * pitch, pitch), pitch)
        got[t, own, :] = mine[t, own, :]

    def slot(ref, p):
        size = ref.shape[0] // chips
        return ref.at[pl.ds(pl.multiple_of(p * size, size), size)]

    def merge_chips(t):
        for d in offsets:
            src = behind(d)
            remote(slot(got.at[t], src), slot(got.at[t], src), s1.at[t, src], r1.at[t, src], partner).wait_recv()
        s = got[t, pl.ds(share, chips, stride=pitch), :]
        w = jnp.exp(s - jnp.max(s, axis=0, keepdims=True))
        w = w / jnp.sum(other(s) * w, axis=0, keepdims=True)
        wt = w.T
        mid = slice(t * share, (t + 1) * share)
        out = got[t, :share, :] * wt[mid, 0:1]
        for p in range(1, chips):
            out = out + got[t, p * pitch:p * pitch + share, :] * wt[mid, p:p + 1]
        return out.astype(BF16)

    each = groups // halves
    for t in range(halves):
        stats = jnp.zeros((rows, wide), F32)
        early = each // 2 if t else 0
        if t:
            stats = lax.fori_loop(t * each, t * each + early, attend, stats)
            merge_pair(t - 1)
        stats = lax.fori_loop(t * each + early, (t + 1) * each, attend, stats)
        o_ref[pl.ds(t * rows * pitch + share, rows, stride=pitch), :] = stats
        swap(t).start()
    merge_pair(halves - 1)
    out = jnp.concatenate([merge_chips(t) for t in range(halves)], axis=0)
    get_wo.wait()
    for p in range(chips):
        r = jnp.dot(out, wo[:, p * 2 * wide:(p + 1) * 2 * wide], preferred_element_type=F32)
        part[0, p * batch:(p + 1) * batch, :] = r[:, :wide]
        part[1, p * batch:(p + 1) * batch, :] = r[:, wide:]
    swap2 = remote(part.at[1 - core], ptheirs, xs.at[halves], xr.at[halves], partner)
    swap2.start()
    swap2.wait_recv()
    pmine[...] = part[core] + ptheirs[...]
    for d in offsets:
        to = ahead(d)
        cp = remote(slot(pmine, to), slot(pgot, chip), s2.at[to], r2.at[chip], to * 2 + core)
        cp.start()
        started.append(cp)
    own = pl.ds(pl.multiple_of(chip * batch, batch), batch)
    pgot[own, :] = pmine[own, :]
    for d in offsets:
        src = behind(d)
        remote(slot(pgot, src), slot(pgot, src), s2.at[src], r2.at[src], partner).wait_recv()
    y = pgot[:batch, :]
    for p in range(1, chips):
        y = y + pgot[p * batch:(p + 1) * batch, :]
    y_ref[:, pl.ds(pl.multiple_of(me * wide, wide), wide)] = y.astype(BF16)

    def block(c, p):
        return y_ref.at[:, pl.ds(pl.multiple_of((p * 2 + c) * wide, wide), wide)]

    started += gather_blocks(block, chip, core, offsets, ahead, behind, (send, recv, fsend, frecv))
    for t in range(halves):
        swap(t).wait_send()
    swap2.wait_send()
    for cp in started:
        cp.wait_send()


def store_kernel(pos_ref, k_ref, v_ref, kn_ref, vn_ref, y_ref, ko_ref, vo_ref, yo_ref, sem, rsem, ysem):
    batch, length = k_ref.shape[:2]
    chunks = sem.shape[1]
    per = batch // chunks
    base = lax.axis_index('seq') * length

    def whole(src, dst, a, i):
        return pltpu.make_async_copy(src.at[pl.ds(i * per, per)], dst.at[pl.ds(i * per, per)], sem.at[a, i])

    def row(src, dst, a, b):
        at = jnp.clip(pos_ref[b] - base, 0, length - 1)
        return pltpu.make_async_copy(src.at[b], dst.at[b, at], rsem.at[a, b])

    def here(b):
        end = pos_ref[b] - base
        return (end >= 0) & (end < length)

    @pl.loop(0, chunks)
    def _(i):
        whole(k_ref, ko_ref, 0, i).start()
        whole(v_ref, vo_ref, 1, i).start()

    y = pltpu.make_async_copy(y_ref, yo_ref, ysem)
    y.start()

    @pl.loop(0, chunks)
    def _(i):
        whole(k_ref, ko_ref, 0, i).wait()
        whole(v_ref, vo_ref, 1, i).wait()
        for j in range(per):
            b = i * per + j

            @pl.when(here(b))
            def _():
                row(kn_ref, ko_ref, 0, b).start()
                row(vn_ref, vo_ref, 1, b).start()

    y.wait()

    @pl.loop(0, batch)
    def _(b):
        @pl.when(here(b))
        def _():
            row(kn_ref, ko_ref, 0, b).wait()
            row(vn_ref, vo_ref, 1, b).wait()


def solution(mesh):
    n = mesh.shape['seq']
    chips = n // 2
    cache_spec = P('rep', 'seq', None, None)
    in_specs = (P('rep', None), P(), P(), P(), P('seq', None), cache_spec, cache_spec, P('rep'))
    out_specs = (P('rep', None), cache_spec, cache_spec)
    vmem = pl.BlockSpec(memory_space=pltpu.VMEM)
    smem = pl.BlockSpec(memory_space=pltpu.SMEM)
    hbm = pl.BlockSpec(memory_space=pltpu.HBM)
    anywhere = pl.BlockSpec(memory_space=pl.ANY)

    def step(x, wq, wk, wv, wo, k, v, pos):
        batch, depth = x.shape
        length, kv_heads, wide = k.shape[1:]
        heads = wq.shape[1] // wide
        slots = DMA((chips,))
        per = 2 * wide // heads
        groups = batch // per
        halves = 2
        pitch = batch // halves + 8
        cache = VMEM((groups, per, length, kv_heads, wide), BF16)
        new = jax.ShapeDtypeStruct((batch, kv_heads, wide), BF16)
        y, kn, vn = pl.pallas_call(
            functools.partial(decode_kernel, n),
            out_shape=[jax.ShapeDtypeStruct((batch, depth), BF16), new, new],
            in_specs=[anywhere] * 8, out_specs=[vmem] * 3,
            scratch_shapes=[
                pltpu.SMEM((batch,), jnp.int32), VMEM((batch, depth), BF16), VMEM(wo.shape, BF16),
                VMEM((depth, 2 * wide), BF16), VMEM((2, chips, batch + batch // 2, wide), BF16), cache, cache,
                VMEM((batch * heads, wide), F32), VMEM((2 * batch * kv_heads, wide), F32),
                VMEM((halves * heads * pitch, wide), F32)]
            + [VMEM((halves, chips * pitch, wide), F32)] * 3 + [VMEM((2, chips * batch, wide), F32)]
            + [VMEM((chips * batch, wide), F32)] * 3 + [DMA((3,)), DMA((2, 4)), DMA((2, groups))] + [slots] * 4
            + [DMA((halves + 1,))] * 2 + [DMA((halves, chips))] * 2 + [slots] * 6,
            compiler_params=pltpu.CompilerParams(collective_id=0, has_side_effects=True, vmem_limit_bytes=45 << 20),
            cost_estimate=pl.CostEstimate(flops=10 ** 10, bytes_accessed=32 << 20, transcendentals=0),
            name='decode',
        )(*(pltpu.with_memory_space_constraint(a, pltpu.HBM) for a in (pos, x, wq, wk, wv, wo, k, v)))
        chunks = 16
        ko, vo, y = pl.pallas_call(
            store_kernel,
            out_shape=[jax.ShapeDtypeStruct(k.shape, k.dtype), jax.ShapeDtypeStruct(v.shape, v.dtype),
                       jax.ShapeDtypeStruct((batch, depth), BF16)],
            in_specs=[smem, anywhere, anywhere, vmem, vmem, vmem], out_specs=[hbm, hbm, hbm],
            scratch_shapes=[DMA((2, chunks)), DMA((2, batch)), DMA],
            compiler_params=pltpu.CompilerParams(vmem_limit_bytes=4 << 20),
            cost_estimate=pl.CostEstimate(flops=10 ** 8, bytes_accessed=32 << 20, transcendentals=0),
            name='store',
        )(pos, k, v, kn, vn, y)
        return y, ko, vo

    return jax.shard_map(step, mesh=mesh, in_specs=in_specs, out_specs=out_specs, check_vma=False)
```

time: 75.7 us -> 67.4 us (0.89)
  Pallas kernels: 71.9 us -> 66.6 us
  local copies, waits for them, and re-layouts: 2.92 us -> 0.01 us
    pallas_call x1, Pallas kernels: 64 us -> 58.7 us  [step(): pl.pallas_call(functools.partial(decode_kernel, n), out_shape=[jax.ShapeD...]
    unnamed x10 -> x6, local copies, waits for them, and re-layouts: 2.92 us -> 0.01 us
where the time goes in v3:
time: 67.4 us; the launch traced here: 67.3 us
  Pallas kernels  66.6 us (99%)
  between operations  0.69 us (1%)
    pallas_call x1, Pallas kernels, step(): pl.pallas_call(functools.partial(decode_kernel, n), out_shape=[jax.ShapeD...  58.7 us
    pallas_call x1, Pallas kernels, step(): pl.pallas_call(store_kernel, out_shape=[jax.ShapeDtypeStruct(k.shape, k.d...  7.94 us

profile of v3, /device:TPU:97, one launch (start us, length us, event | category | flops | bytes accessed | tf_op | source)
XLA Modules:
  0.0 67.3 jit_solution(2039782567473718660)
XLA Ops:
  0.6 0.0 copy-start.2
  0.6 0.0 copy-start.1
  0.7 0.0 copy-start
  0.7 58.7 %decode.1 = (bf16[64,4096]{1,0:T(8,128)(2,1)S(1)}, bf16[64,8,128]{2,1,0:T(8,128)(2,1)S(1)}, bf16[64,8,128]{2,1,0:T(8,128)(2,1)S(1)}) custom-call(s32[64]{0:T(128)} %pos_ref.3, bf16[64,4096]{1,0:T(8,128)(2,1)} %x_ref.1, bf16[4096,4096]{1,0:T(8,128)(2,1)} %wq_ref.1, bf16[4096,1024]{1,0:T(8,128)(2,1)} %wk_ref.1, bf16[4096,1024]{1,0:T(8,128)(2,1)} %wv_ref.1, ...), custom_call_target="tpu_custom_call" | custom-call | flops 10000000000 | bytes 33554432 | tf_op jit(solution)/shard_map/decode/pallas_call | solution.py:379
  59.4 0.0 copy-done.2
  59.4 0.0 copy-done.1
  59.4 0.0 copy-done
  59.4 7.9 %store.1 = (bf16[64,64,8,128]{3,2,1,0:T(8,128)(2,1)}, bf16[64,64,8,128]{3,2,1,0:T(8,128)(2,1)}, bf16[64,4096]{1,0:T(8,128)(2,1)}) custom-call(s32[64]{0:T(128)S(1)} %copy-done.2, bf16[64,64,8,128]{3,2,1,0:T(8,128)(2,1)S(1)} %copy-done, bf16[64,64,8,128]{3,2,1,0:T(8,128)(2,1)S(1)} %copy-done.1, bf16[64,8,128]{2,1,0:T(8,128)(2,1)S(1)} %get-tuple-element.9.kn_ref, ...), custom_call_target="tpu_custom_call" | custom-call | flops 100000000 | bytes 33554432 | tf_op jit(solution)/shard_map/store/pallas_call | solution.py:396
Async XLA Ops:
  0.6 58.7 %copy-start.2 = (s32[64]{0:T(128)S(1)}, s32[64]{0:T(128)}, u32[]{:S(2)}) copy-start(s32[64]{0:T(128)} %pos_ref.3) | copy-start | bytes 772
  0.6 58.7 %copy-start.1 = (bf16[64,64,8,128]{3,2,1,0:T(8,128)(2,1)S(1)}, bf16[64,64,8,128]{3,2,1,0:T(8,128)(2,1)}, u32[]{:S(2)}) copy-start(bf16[64,64,8,128]{3,2,1,0:T(8,128)(2,1)} %v_ref.3) | copy-start | bytes 25165828
  0.7 58.7 %copy-start = (bf16[64,64,8,128]{3,2,1,0:T(8,128)(2,1)S(1)}, bf16[64,64,8,128]{3,2,1,0:T(8,128)(2,1)}, u32[]{:S(2)}) copy-start(bf16[64,64,8,128]{3,2,1,0:T(8,128)(2,1)} %k_ref.3) | copy-start | bytes 25165828

commit v4 on v3

--- a/solution.py
+++ b/solution.py
@@ -81,7 +81,7 @@
 
 
 def decode_kernel(n, pos_ref, x_ref, wq_ref, wk_ref, wv_ref, wo_ref, k_ref, v_ref, y_ref, kn_ref, vn_ref,
-                  pos, x, wo, wbuf, g_ref, kbuf, vbuf, qf, kvf, o_ref, theirs, mine, got, part, ptheirs, pmine, pgot,
+                  pos, x, wo, wbuf, g_ref, kbuf, vbuf, qf, kvf, raw, wts, mls, o_ref, theirs, mine, got, part, ptheirs, pmine, pgot,
                   isem, wsem, ksem, asend, arecv, afsend, afrecv, xs, xr, s1, r1, s2, r2, send, recv, fsend, frecv):
     me, chip, core, offsets, ahead, behind = place(n)
     chips = n // 2
@@ -165,48 +165,64 @@
     qlane = lax.broadcasted_iota(jnp.int32, (wide, lanes), 1) // rows
     slane = lax.broadcasted_iota(jnp.int32, (rows, wide), 1)
 
-    def attend(i, stats):
+    zero = jnp.zeros((kv_heads, 2 * wide), BF16)
+
+    def fresh(i, j, which):
+        at = (which * batch + i * per + j) * kv_heads
+        return kvf[pl.ds(pl.multiple_of(at, kv_heads), kv_heads), :].astype(BF16)
+
+    def scores(i, slot):
         k_in(i).wait()
-        v_in(i).wait()
-        end = jnp.zeros((kv_heads, lanes), jnp.int32)
-        fresh = []
         for j in range(per):
-            b = i * per + j
-            end = jnp.where(member == j, pos[b] - base, end)
-            kn = kvf[pl.ds(pl.multiple_of(b * kv_heads, kv_heads), kv_heads), :].astype(BF16)
-            vn = kvf[pl.ds(pl.multiple_of((batch + b) * kv_heads, kv_heads), kv_heads), :].astype(BF16)
-            kn_ref[b] = kn
-            vn_ref[b] = vn
-            fresh.append((kn, vn))
+            kn_ref[i * per + j] = fresh(i, j, 0)
         qt = qf[pl.ds(pl.multiple_of(i * lanes, lanes), lanes), :].T.astype(BF16)
         query = jnp.concatenate([jnp.where(qlane == j, qt, 0) for j in range(per)], axis=0)
         keys = jnp.concatenate([kbuf[i, j].reshape(cols, wide) for j in range(per)], axis=1)
+        raw[slot, :cols, :] = jnp.dot(keys, query, preferred_element_type=F32)
+        raw[slot, cols:, :] = jnp.dot(jnp.concatenate([fresh(i, j, 0) for j in range(per)], axis=1), query,
+                                      preferred_element_type=F32)
+
+    def soften(i, slot):
+        end = jnp.zeros((kv_heads, lanes), jnp.int32)
+        for j in range(per):
+            end = jnp.where(member == j, pos[i * per + j] - base, end)
         scale = wide ** -0.5
-        s = jnp.dot(keys, query, preferred_element_type=F32).reshape(length, kv_heads, lanes) * scale
-        newest = jnp.dot(jnp.concatenate([f[0] for f in fresh], axis=1), query, preferred_element_type=F32) * scale
         t = lax.broadcasted_iota(jnp.int32, (length, kv_heads, lanes), 0)
+        s = raw[slot, :cols, :].reshape(length, kv_heads, lanes) * scale
         s = jnp.where(t < jnp.where(ours, end, 0)[None], s, -jnp.inf)
-        newest = jnp.where(ours & (end >= 0) & (end < length), newest, -jnp.inf)
+        newest = jnp.where(ours & (end >= 0) & (end < length), raw[slot, cols:, :] * scale, -jnp.inf)
         m = jnp.max(jnp.maximum(jnp.max(s, axis=0), newest), axis=0, keepdims=True)
         safe = jnp.where(m == -jnp.inf, 0.0, m)
         w = jnp.exp(s - safe[None])
         nw = jnp.exp(newest - safe)
         total = jnp.sum(jnp.sum(w, axis=0) + nw, axis=0, keepdims=True)
-        wt = w.reshape(cols, lanes).T.astype(BF16)
-        extra = jnp.concatenate([nw, m, total, jnp.zeros((kv_heads - 2, lanes), F32)], axis=0).T
+        wts[slot, :, :cols] = w.reshape(cols, lanes).T.astype(BF16)
+        wts[slot, :, cols:] = jnp.concatenate([nw, jnp.zeros((wide - kv_heads, lanes), F32)], axis=0).T.astype(BF16)
+        mls[slot] = jnp.concatenate([m, total, jnp.zeros((kv_heads - 2, lanes), F32)], axis=0).T
+
+    def values(i, slot, stats):
+        v_in(i).wait()
         at = (i // (groups // halves)) * rows * pitch + (i % (groups // halves)) * per
         for j in range(0, per, 2):
-            both = slice(j * rows, (j + 2) * rows)
+            vn0, vn1 = fresh(i, j, 1), fresh(i, j + 1, 1)
+            vn_ref[i * per + j] = vn0
+            vn_ref[i * per + j + 1] = vn1
             vals = jnp.concatenate([vbuf[i, j].reshape(cols, wide), vbuf[i, j + 1].reshape(cols, wide)], axis=1)
-            news = jnp.concatenate([fresh[j][1], fresh[j + 1][1]], axis=1)
-            o = jnp.dot(wt[both], vals, preferred_element_type=F32)
-            o = o + jnp.dot(extra[both, :kv_heads].astype(BF16), news, preferred_element_type=F32)
+            vals = jnp.concatenate([vals, jnp.concatenate([vn0, vn1], axis=1), zero], axis=0)
+            o = jnp.dot(wts[slot, j * rows:(j + 2) * rows, :cols + 2 * kv_heads], vals, preferred_element_type=F32)
             o_ref[pl.ds(at + j, rows, stride=pitch), :] = o[:rows, :wide]
             o_ref[pl.ds(at + j + 1, rows, stride=pitch), :] = o[rows:, wide:]
         for j in range(per):
-            z = extra[j * rows:(j + 1) * rows, :]
-            stats = jnp.where(slane == i * per + j, z[:, kv_heads:kv_heads + 1], stats)
-            stats = jnp.where(slane == batch + i * per + j, z[:, kv_heads + 1:kv_heads + 2], stats)
+            z = mls[slot, j * rows:(j + 1) * rows, :]
+            stats = jnp.where(slane == i * per + j, z[:, 0:1], stats)
+            stats = jnp.where(slane == batch + i * per + j, z[:, 1:2], stats)
+        return stats
+
+    def attend(p, stats):
+        for c in range(2):
+            stats = values(2 * p + c, c, stats)
+            soften(2 * p + c + 1, 1 - c)
+            scores(2 * p + c + 2, c)
         return stats
 
     def other(v):
@@ -260,17 +276,23 @@
             out = out + got[t, p * pitch:p * pitch + share, :] * wt[mid, p:p + 1]
         return out.astype(BF16)
 
-    each = groups // halves
-    for t in range(halves):
-        stats = jnp.zeros((rows, wide), F32)
-        early = each // 2 if t else 0
-        if t:
-            stats = lax.fori_loop(t * each, t * each + early, attend, stats)
-            merge_pair(t - 1)
-        stats = lax.fori_loop(t * each + early, (t + 1) * each, attend, stats)
+    pairs = groups // 2
+    none = jnp.zeros((rows, wide), F32)
+    scores(0, 0)
+    soften(0, 0)
+    scores(1, 1)
+
+    def finish(t, stats):
         o_ref[pl.ds(t * rows * pitch + share, rows, stride=pitch), :] = stats
         swap(t).start()
-    merge_pair(halves - 1)
+
+    finish(0, lax.fori_loop(0, pairs // 2, attend, none))
+    stats = lax.fori_loop(pairs // 2, pairs - 1, attend, none)
+    merge_pair(0)
+    stats = values(groups - 2, 0, stats)
+    soften(groups - 1, 1)
+    finish(1, values(groups - 1, 1, stats))
+    merge_pair(1)
     out = jnp.concatenate([merge_chips(t) for t in range(halves)], axis=0)
     get_wo.wait()
     for p in range(chips):
@@ -384,6 +406,8 @@
                 pltpu.SMEM((batch,), jnp.int32), VMEM((batch, depth), BF16), VMEM(wo.shape, BF16),
                 VMEM((depth, 2 * wide), BF16), VMEM((2, chips, batch + batch // 2, wide), BF16), cache, cache,
                 VMEM((batch * heads, wide), F32), VMEM((2 * batch * kv_heads, wide), F32),
+                VMEM((2, (length + 1) * kv_heads, per * heads), F32),
+                VMEM((2, per * heads, length * kv_heads + wide), BF16), VMEM((2, per * heads, kv_heads), F32),
                 VMEM((halves * heads * pitch, wide), F32)]
             + [VMEM((halves, chips * pitch, wide), F32)] * 3 + [VMEM((2, chips * batch, wide), F32)]
             + [VMEM((chips * batch, wide), F32)] * 3 + [DMA((3,)), DMA((2, 4)), DMA((2, groups))] + [slots] * 4

time: 67.4 us -> 67.1 us (level)
  no operation moved by 1% of the time
where the time goes in v4:
time: 67.1 us; the launch traced here: 67 us
  Pallas kernels  66.3 us (99%)
  between operations  0.69 us (1%)
    pallas_call x1, Pallas kernels, step(): pl.pallas_call(functools.partial(decode_kernel, n), out_shape=[jax.ShapeD...  58.4 us
    pallas_call x1, Pallas kernels, step(): pl.pallas_call(store_kernel, out_shape=[jax.ShapeDtypeStruct(k.shape, k.d...  7.94 us

profile of v4, /device:TPU:97, one launch (start us, length us, event | category | flops | bytes accessed | tf_op | source)
XLA Modules:
  0.0 67.0 jit_solution(17607175920310643671)
XLA Ops:
  0.6 0.0 copy-start.2
  0.6 0.0 copy-start.1
  0.7 0.0 copy-start
  0.7 58.4 %decode.1 = (bf16[64,4096]{1,0:T(8,128)(2,1)S(1)}, bf16[64,8,128]{2,1,0:T(8,128)(2,1)S(1)}, bf16[64,8,128]{2,1,0:T(8,128)(2,1)S(1)}) custom-call(s32[64]{0:T(128)} %pos_ref.3, bf16[64,4096]{1,0:T(8,128)(2,1)} %x_ref.1, bf16[4096,4096]{1,0:T(8,128)(2,1)} %wq_ref.1, bf16[4096,1024]{1,0:T(8,128)(2,1)} %wk_ref.1, bf16[4096,1024]{1,0:T(8,128)(2,1)} %wv_ref.1, ...), custom_call_target="tpu_custom_call" | custom-call | flops 10000000000 | bytes 33554432 | tf_op jit(solution)/shard_map/decode/pallas_call | solution.py:401
  59.0 0.0 copy-done.2
  59.0 0.0 copy-done.1
  59.0 0.0 copy-done
  59.1 7.9 %store.1 = (bf16[64,64,8,128]{3,2,1,0:T(8,128)(2,1)}, bf16[64,64,8,128]{3,2,1,0:T(8,128)(2,1)}, bf16[64,4096]{1,0:T(8,128)(2,1)}) custom-call(s32[64]{0:T(128)S(1)} %copy-done.2, bf16[64,64,8,128]{3,2,1,0:T(8,128)(2,1)S(1)} %copy-done, bf16[64,64,8,128]{3,2,1,0:T(8,128)(2,1)S(1)} %copy-done.1, bf16[64,8,128]{2,1,0:T(8,128)(2,1)S(1)} %get-tuple-element.9.kn_ref, ...), custom_call_target="tpu_custom_call" | custom-call | flops 100000000 | bytes 33554432 | tf_op jit(solution)/shard_map/store/pallas_call | solution.py:420
Async XLA Ops:
  0.6 58.4 %copy-start.2 = (s32[64]{0:T(128)S(1)}, s32[64]{0:T(128)}, u32[]{:S(2)}) copy-start(s32[64]{0:T(128)} %pos_ref.3) | copy-start | bytes 772
  0.6 58.4 %copy-start.1 = (bf16[64,64,8,128]{3,2,1,0:T(8,128)(2,1)S(1)}, bf16[64,64,8,128]{3,2,1,0:T(8,128)(2,1)}, u32[]{:S(2)}) copy-start(bf16[64,64,8,128]{3,2,1,0:T(8,128)(2,1)} %v_ref.3) | copy-start | bytes 25165828
  0.7 58.4 %copy-start = (bf16[64,64,8,128]{3,2,1,0:T(8,128)(2,1)S(1)}, bf16[64,64,8,128]{3,2,1,0:T(8,128)(2,1)}, u32[]{:S(2)}) copy-start(bf16[64,64,8,128]{3,2,1,0:T(8,128)(2,1)} %k_ref.3) | copy-start | bytes 25165828

commit v5 on v4

--- a/solution.py
+++ b/solution.py
@@ -50,7 +50,7 @@
     return barrier
 
 
-def gather_blocks(block, chip, core, offsets, ahead, behind, sems, took=None):
+def gather_blocks(block, chip, core, offsets, ahead, behind, sems, took=None, between=None):
     send, recv, fsend, frecv = sems
     partner = chip * 2 + 1 - core
     started = []
@@ -63,7 +63,9 @@
     started.append(cp)
     if took is not None:
         took(core, chip)
-    for d in offsets:
+    for k, d in enumerate(offsets):
+        if k == 5 and between is not None:
+            started += between()
         src = behind(d)
         got = block(core, src)
         remote(got, got, send.at[src], recv.at[src], partner).wait_recv()
@@ -81,8 +83,8 @@
 
 
 def decode_kernel(n, pos_ref, x_ref, wq_ref, wk_ref, wv_ref, wo_ref, k_ref, v_ref, y_ref, kn_ref, vn_ref,
-                  pos, x, wo, wbuf, g_ref, kbuf, vbuf, qf, kvf, raw, wts, mls, o_ref, theirs, mine, got, part, ptheirs, pmine, pgot,
-                  isem, wsem, ksem, asend, arecv, afsend, afrecv, xs, xr, s1, r1, s2, r2, send, recv, fsend, frecv):
+                  pos, x, wo, wbuf, g_ref, kbuf, vbuf, qf, kvf, raw, wts, mls, o_ref, theirs, mine, got, wcol, heads, part, ptheirs,
+                  isem, wsem, ksem, asend, arecv, afsend, afrecv, xs, xr, s1, r1, s2, r2, s3, r3, send, recv, fsend, frecv):
     me, chip, core, offsets, ahead, behind = place(n)
     chips = n // 2
     partner = chip * 2 + 1 - core
@@ -152,8 +154,22 @@
         at = (p // kv_heads) * batch * kv_heads + c * half * kv_heads + p % kv_heads
         kvf[pl.ds(at, half, stride=kv_heads), :] = g_ref[c, p, batch:, :].astype(F32)
 
+    def columns(p):
+        return pl.ds(pl.multiple_of(p * 2 * wide, 2 * wide), 2 * wide)
+
+    def spread():
+        get_wo.wait()
+        cps = []
+        for d in offsets:
+            to = ahead(d)
+            cp = remote(wo.at[:, columns(to)], wcol.at[chip], s3.at[to], r3.at[chip], to * 2 + core)
+            cp.start()
+            cps.append(cp)
+        wcol[chip] = wo[:, columns(chip)]
+        return cps
+
     started = gather_blocks(lambda c, p: g_ref.at[c, p], chip, core, offsets, ahead, behind,
-                            (asend, arecv, afsend, afrecv), took)
+                            (asend, arecv, afsend, afrecv), took, spread)
     get_pos.wait()
 
     cols = length * kv_heads
@@ -294,28 +310,26 @@
     finish(1, values(groups - 1, 1, stats))
     merge_pair(1)
     out = jnp.concatenate([merge_chips(t) for t in range(halves)], axis=0)
-    get_wo.wait()
-    for p in range(chips):
-        r = jnp.dot(out, wo[:, p * 2 * wide:(p + 1) * 2 * wide], preferred_element_type=F32)
-        part[0, p * batch:(p + 1) * batch, :] = r[:, :wide]
-        part[1, p * batch:(p + 1) * batch, :] = r[:, wide:]
+    heads[chip] = out
+    for d in offsets:
+        to = ahead(d)
+        cp = remote(heads.at[chip], heads.at[chip], s2.at[to], r2.at[chip], to * 2 + core)
+        cp.start()
+        started.append(cp)
+    for d in offsets:
+        src = behind(d)
+        remote(wcol.at[src], wcol.at[src], s3.at[src], r3.at[src], partner).wait_recv()
+    for d in offsets:
+        src = behind(d)
+        remote(heads.at[src], heads.at[src], s2.at[src], r2.at[src], partner).wait_recv()
+    y = jnp.dot(jnp.concatenate([heads[p] for p in range(chips)], axis=1), wcol[...].reshape(chips * wide, 2 * wide),
+                preferred_element_type=F32)
+    part[0] = y[:, :wide]
+    part[1] = y[:, wide:]
     swap2 = remote(part.at[1 - core], ptheirs, xs.at[halves], xr.at[halves], partner)
     swap2.start()
     swap2.wait_recv()
-    pmine[...] = part[core] + ptheirs[...]
-    for d in offsets:
-        to = ahead(d)
-        cp = remote(slot(pmine, to), slot(pgot, chip), s2.at[to], r2.at[chip], to * 2 + core)
-        cp.start()
-        started.append(cp)
-    own = pl.ds(pl.multiple_of(chip * batch, batch), batch)
-    pgot[own, :] = pmine[own, :]
-    for d in offsets:
-        src = behind(d)
-        remote(slot(pgot, src), slot(pgot, src), s2.at[src], r2.at[src], partner).wait_recv()
-    y = pgot[:batch, :]
-    for p in range(1, chips):
-        y = y + pgot[p * batch:(p + 1) * batch, :]
+    y = part[core] + ptheirs[...]
     y_ref[:, pl.ds(pl.multiple_of(me * wide, wide), wide)] = y.astype(BF16)
 
     def block(c, p):
@@ -409,9 +423,10 @@
                 VMEM((2, (length + 1) * kv_heads, per * heads), F32),
                 VMEM((2, per * heads, length * kv_heads + wide), BF16), VMEM((2, per * heads, kv_heads), F32),
                 VMEM((halves * heads * pitch, wide), F32)]
-            + [VMEM((halves, chips * pitch, wide), F32)] * 3 + [VMEM((2, chips * batch, wide), F32)]
-            + [VMEM((chips * batch, wide), F32)] * 3 + [DMA((3,)), DMA((2, 4)), DMA((2, groups))] + [slots] * 4
-            + [DMA((halves + 1,))] * 2 + [DMA((halves, chips))] * 2 + [slots] * 6,
+            + [VMEM((halves, chips * pitch, wide), F32)] * 3
+            + [VMEM((chips, wide, 2 * wide), BF16), VMEM((chips, batch, wide), BF16), VMEM((2, batch, wide), F32),
+               VMEM((batch, wide), F32)] + [DMA((3,)), DMA((2, 4)), DMA((2, groups))] + [slots] * 4
+            + [DMA((halves + 1,))] * 2 + [DMA((halves, chips))] * 2 + [slots] * 8,
             compiler_params=pltpu.CompilerParams(collective_id=0, has_side_effects=True, vmem_limit_bytes=45 << 20),
             cost_estimate=pl.CostEstimate(flops=10 ** 10, bytes_accessed=32 << 20, transcendentals=0),
             name='decode',

time: 67.1 us -> 64.6 us (0.963)
  Pallas kernels: 66.3 us -> 63.8 us
    pallas_call x1, Pallas kernels: 58.4 us -> 55.9 us  [step(): pl.pallas_call(functools.partial(decode_kernel, n), out_shape=[jax.ShapeD...]
where the time goes in v5:
time: 64.6 us; the launch traced here: 64.5 us
  Pallas kernels  63.8 us (99%)
  between operations  0.69 us (1%)
    pallas_call x1, Pallas kernels, step(): pl.pallas_call(functools.partial(decode_kernel, n), out_shape=[jax.ShapeD...  55.9 us
    pallas_call x1, Pallas kernels, step(): pl.pallas_call(store_kernel, out_shape=[jax.ShapeDtypeStruct(k.shape, k.d...  7.94 us

profile of v5, /device:TPU:97, one launch (start us, length us, event | category | flops | bytes accessed | tf_op | source)
XLA Modules:
  0.0 64.5 jit_solution(190453201943818483)
XLA Ops:
  0.6 0.0 copy-start.2
  0.6 0.0 copy-start.1
  0.7 0.0 copy-start
  0.7 55.9 %decode.1 = (bf16[64,4096]{1,0:T(8,128)(2,1)S(1)}, bf16[64,8,128]{2,1,0:T(8,128)(2,1)S(1)}, bf16[64,8,128]{2,1,0:T(8,128)(2,1)S(1)}) custom-call(s32[64]{0:T(128)} %pos_ref.3, bf16[64,4096]{1,0:T(8,128)(2,1)} %x_ref.1, bf16[4096,4096]{1,0:T(8,128)(2,1)} %wq_ref.1, bf16[4096,1024]{1,0:T(8,128)(2,1)} %wk_ref.1, bf16[4096,1024]{1,0:T(8,128)(2,1)} %wv_ref.1, ...), custom_call_target="tpu_custom_call" | custom-call | flops 10000000000 | bytes 33554432 | tf_op jit(solution)/shard_map/decode/pallas_call | solution.py:415
  56.5 0.0 copy-done.2
  56.6 0.0 copy-done.1
  56.6 0.0 copy-done
  56.6 7.9 %store.1 = (bf16[64,64,8,128]{3,2,1,0:T(8,128)(2,1)}, bf16[64,64,8,128]{3,2,1,0:T(8,128)(2,1)}, bf16[64,4096]{1,0:T(8,128)(2,1)}) custom-call(s32[64]{0:T(128)S(1)} %copy-done.2, bf16[64,64,8,128]{3,2,1,0:T(8,128)(2,1)S(1)} %copy-done, bf16[64,64,8,128]{3,2,1,0:T(8,128)(2,1)S(1)} %copy-done.1, bf16[64,8,128]{2,1,0:T(8,128)(2,1)S(1)} %get-tuple-element.9.kn_ref, ...), custom_call_target="tpu_custom_call" | custom-call | flops 100000000 | bytes 33554432 | tf_op jit(solution)/shard_map/store/pallas_call | solution.py:435
Async XLA Ops:
  0.6 55.9 %copy-start.2 = (s32[64]{0:T(128)S(1)}, s32[64]{0:T(128)}, u32[]{:S(2)}) copy-start(s32[64]{0:T(128)} %pos_ref.3) | copy-start | bytes 772
  0.6 55.9 %copy-start.1 = (bf16[64,64,8,128]{3,2,1,0:T(8,128)(2,1)S(1)}, bf16[64,64,8,128]{3,2,1,0:T(8,128)(2,1)}, u32[]{:S(2)}) copy-start(bf16[64,64,8,128]{3,2,1,0:T(8,128)(2,1)} %v_ref.3) | copy-start | bytes 25165828
  0.7 55.9 %copy-start = (bf16[64,64,8,128]{3,2,1,0:T(8,128)(2,1)S(1)}, bf16[64,64,8,128]{3,2,1,0:T(8,128)(2,1)}, u32[]{:S(2)}) copy-start(bf16[64,64,8,128]{3,2,1,0:T(8,128)(2,1)} %k_ref.3) | copy-start | bytes 25165828

commit v6 on v5

--- a/solution.py
+++ b/solution.py
@@ -63,7 +63,7 @@
     started.append(cp)
     if took is not None:
         took(core, chip)
-    for k, d in enumerate(offsets):
+    for k, d in enumerate(reversed(offsets)):
         if k == 5 and between is not None:
             started += between()
         src = behind(d)
@@ -74,7 +74,7 @@
         started.append(cp)
         if took is not None:
             took(core, src)
-    for src in [chip] + [behind(d) for d in offsets]:
+    for src in [chip] + [behind(d) for d in reversed(offsets)]:
         got = block(1 - core, src)
         remote(got, got, fsend.at[src], frecv.at[src], partner).wait_recv()
         if took is not None:

time: 64.6 us -> 63.8 us (0.988)
  Pallas kernels: 63.8 us -> 63 us
    pallas_call x1, Pallas kernels: 55.9 us -> 55.1 us  [step(): pl.pallas_call(functools.partial(decode_kernel, n), out_shape=[jax.ShapeD...]
where the time goes in v6:
time: 63.8 us; the launch traced here: 63.7 us
  Pallas kernels  63 us (99%)
  between operations  0.69 us (1%)
    pallas_call x1, Pallas kernels, step(): pl.pallas_call(functools.partial(decode_kernel, n), out_shape=[jax.ShapeD...  55.1 us
    pallas_call x1, Pallas kernels, step(): pl.pallas_call(store_kernel, out_shape=[jax.ShapeDtypeStruct(k.shape, k.d...  7.94 us

profile of v6, /device:TPU:97, one launch (start us, length us, event | category | flops | bytes accessed | tf_op | source)
XLA Modules:
  0.0 63.7 jit_solution(10937951975303963846)
XLA Ops:
  0.6 0.0 copy-start.2
  0.6 0.0 copy-start.1
  0.7 0.0 copy-start
  0.7 55.1 %decode.1 = (bf16[64,4096]{1,0:T(8,128)(2,1)S(1)}, bf16[64,8,128]{2,1,0:T(8,128)(2,1)S(1)}, bf16[64,8,128]{2,1,0:T(8,128)(2,1)S(1)}) custom-call(s32[64]{0:T(128)} %pos_ref.3, bf16[64,4096]{1,0:T(8,128)(2,1)} %x_ref.1, bf16[4096,4096]{1,0:T(8,128)(2,1)} %wq_ref.1, bf16[4096,1024]{1,0:T(8,128)(2,1)} %wk_ref.1, bf16[4096,1024]{1,0:T(8,128)(2,1)} %wv_ref.1, ...), custom_call_target="tpu_custom_call" | custom-call | flops 10000000000 | bytes 33554432 | tf_op jit(solution)/shard_map/decode/pallas_call | solution.py:415
  55.7 0.0 copy-done.2
  55.8 0.0 copy-done.1
  55.8 0.0 copy-done
  55.8 7.9 %store.1 = (bf16[64,64,8,128]{3,2,1,0:T(8,128)(2,1)}, bf16[64,64,8,128]{3,2,1,0:T(8,128)(2,1)}, bf16[64,4096]{1,0:T(8,128)(2,1)}) custom-call(s32[64]{0:T(128)S(1)} %copy-done.2, bf16[64,64,8,128]{3,2,1,0:T(8,128)(2,1)S(1)} %copy-done, bf16[64,64,8,128]{3,2,1,0:T(8,128)(2,1)S(1)} %copy-done.1, bf16[64,8,128]{2,1,0:T(8,128)(2,1)S(1)} %get-tuple-element.9.kn_ref, ...), custom_call_target="tpu_custom_call" | custom-call | flops 100000000 | bytes 33554432 | tf_op jit(solution)/shard_map/store/pallas_call | solution.py:435
Async XLA Ops:
  0.6 55.1 %copy-start.2 = (s32[64]{0:T(128)S(1)}, s32[64]{0:T(128)}, u32[]{:S(2)}) copy-start(s32[64]{0:T(128)} %pos_ref.3) | copy-start | bytes 772
  0.6 55.1 %copy-start.1 = (bf16[64,64,8,128]{3,2,1,0:T(8,128)(2,1)S(1)}, bf16[64,64,8,128]{3,2,1,0:T(8,128)(2,1)}, u32[]{:S(2)}) copy-start(bf16[64,64,8,128]{3,2,1,0:T(8,128)(2,1)} %v_ref.3) | copy-start | bytes 25165828
  0.7 55.1 %copy-start = (bf16[64,64,8,128]{3,2,1,0:T(8,128)(2,1)S(1)}, bf16[64,64,8,128]{3,2,1,0:T(8,128)(2,1)}, u32[]{:S(2)}) copy-start(bf16[64,64,8,128]{3,2,1,0:T(8,128)(2,1)} %k_ref.3) | copy-start | bytes 25165828

commit v7 on v6

--- a/solution.py
+++ b/solution.py
@@ -268,7 +268,7 @@
             mine[t, p * pitch:p * pitch + share, :] = a + b
         for d in offsets:
             to = ahead(d)
-            cp = remote(slot(mine.at[t], to), slot(got.at[t], chip), s1.at[t, to], r1.at[t, chip], to * 2 + core)
+            cp = remote(used(mine.at[t], to), used(got.at[t], chip), s1.at[t, to], r1.at[t, chip], to * 2 + core)
             cp.start()
             started.append(cp)
         own = pl.ds(pl.multiple_of(chip * pitch, pitch), pitch)
@@ -278,10 +278,13 @@
         size = ref.shape[0] // chips
         return ref.at[pl.ds(pl.multiple_of(p * size, size), size)]
 
+    def used(ref, p):
+        return ref.at[pl.ds(pl.multiple_of(p * pitch, pitch), share + 1)]
+
     def merge_chips(t):
         for d in offsets:
             src = behind(d)
-            remote(slot(got.at[t], src), slot(got.at[t], src), s1.at[t, src], r1.at[t, src], partner).wait_recv()
+            remote(used(got.at[t], src), used(got.at[t], src), s1.at[t, src], r1.at[t, src], partner).wait_recv()
         s = got[t, pl.ds(share, chips, stride=pitch), :]
         w = jnp.exp(s - jnp.max(s, axis=0, keepdims=True))
         w = w / jnp.sum(other(s) * w, axis=0, keepdims=True)
@@ -343,7 +346,7 @@
         cp.wait_send()
 
 
-def store_kernel(pos_ref, k_ref, v_ref, kn_ref, vn_ref, y_ref, ko_ref, vo_ref, yo_ref, sem, rsem, ysem):
+def store_kernel(pos_hbm, k_ref, v_ref, kn_ref, vn_ref, y_ref, ko_ref, vo_ref, yo_ref, pos_ref, sem, rsem, ysem):
     batch, length = k_ref.shape[:2]
     chunks = sem.shape[1]
     per = batch // chunks
@@ -365,8 +368,11 @@
         whole(k_ref, ko_ref, 0, i).start()
         whole(v_ref, vo_ref, 1, i).start()
 
-    y = pltpu.make_async_copy(y_ref, yo_ref, ysem)
+    y = pltpu.make_async_copy(y_ref, yo_ref, ysem.at[0])
     y.start()
+    get_pos = pltpu.make_async_copy(pos_hbm, pos_ref, ysem.at[1])
+    get_pos.start()
+    get_pos.wait()
 
     @pl.loop(0, chunks)
     def _(i):
@@ -425,19 +431,19 @@
                 VMEM((halves * heads * pitch, wide), F32)]
             + [VMEM((halves, chips * pitch, wide), F32)] * 3
             + [VMEM((chips, wide, 2 * wide), BF16), VMEM((chips, batch, wide), BF16), VMEM((2, batch, wide), F32),
-               VMEM((batch, wide), F32)] + [DMA((3,)), DMA((2, 4)), DMA((2, groups))] + [slots] * 4
+               VMEM((batch, wide), F32)] + [DMA((3,)), DMA((2, 1)), DMA((2, groups))] + [slots] * 4
             + [DMA((halves + 1,))] * 2 + [DMA((halves, chips))] * 2 + [slots] * 8,
             compiler_params=pltpu.CompilerParams(collective_id=0, has_side_effects=True, vmem_limit_bytes=45 << 20),
             cost_estimate=pl.CostEstimate(flops=10 ** 10, bytes_accessed=32 << 20, transcendentals=0),
             name='decode',
         )(*(pltpu.with_memory_space_constraint(a, pltpu.HBM) for a in (pos, x, wq, wk, wv, wo, k, v)))
-        chunks = 16
+        chunks = 4
         ko, vo, y = pl.pallas_call(
             store_kernel,
             out_shape=[jax.ShapeDtypeStruct(k.shape, k.dtype), jax.ShapeDtypeStruct(v.shape, v.dtype),
                        jax.ShapeDtypeStruct((batch, depth), BF16)],
-            in_specs=[smem, anywhere, anywhere, vmem, vmem, vmem], out_specs=[hbm, hbm, hbm],
-            scratch_shapes=[DMA((2, chunks)), DMA((2, batch)), DMA],
+            in_specs=[anywhere, anywhere, anywhere, vmem, vmem, vmem], out_specs=[hbm, hbm, hbm],
+            scratch_shapes=[pltpu.SMEM((batch,), jnp.int32), DMA((2, chunks)), DMA((2, batch)), DMA((2,))],
             compiler_params=pltpu.CompilerParams(vmem_limit_bytes=4 << 20),
             cost_estimate=pl.CostEstimate(flops=10 ** 8, bytes_accessed=32 << 20, transcendentals=0),
             name='store',

time: 63.8 us -> 61.5 us (0.964)
  Pallas kernels: 63 us -> 60.7 us
    pallas_call x1, Pallas kernels: 55.1 us -> 53.5 us  [step(): pl.pallas_call(functools.partial(decode_kernel, n), out_shape=[jax.ShapeD...]
    pallas_call x1, Pallas kernels: 7.94 us -> 7.2 us  [step(): pl.pallas_call(store_kernel, out_shape=[jax.ShapeDtypeStruct(k.shape, k.d...]
where the time goes in v7:
time: 61.5 us; the launch traced here: 61.4 us
  Pallas kernels  60.7 us (99%)
  between operations  0.69 us (1%)
    pallas_call x1, Pallas kernels, step(): pl.pallas_call(functools.partial(decode_kernel, n), out_shape=[jax.ShapeD...  53.5 us
    pallas_call x1, Pallas kernels, step(): pl.pallas_call(store_kernel, out_shape=[jax.ShapeDtypeStruct(k.shape, k.d...  7.2 us

profile of v7, /device:TPU:97, one launch (start us, length us, event | category | flops | bytes accessed | tf_op | source)
XLA Modules:
  0.0 61.4 jit_solution(15150813504815251491)
XLA Ops:
  0.6 0.0 copy-start.2
  0.6 0.0 copy-start.1
  0.7 0.0 copy-start
  0.7 53.5 %decode.1 = (bf16[64,4096]{1,0:T(8,128)(2,1)S(1)}, bf16[64,8,128]{2,1,0:T(8,128)(2,1)S(1)}, bf16[64,8,128]{2,1,0:T(8,128)(2,1)S(1)}) custom-call(s32[64]{0:T(128)} %pos_hbm.1, bf16[64,4096]{1,0:T(8,128)(2,1)} %x_ref.1, bf16[4096,4096]{1,0:T(8,128)(2,1)} %wq_ref.1, bf16[4096,1024]{1,0:T(8,128)(2,1)} %wk_ref.1, bf16[4096,1024]{1,0:T(8,128)(2,1)} %wv_ref.1, ...), custom_call_target="tpu_custom_call" | custom-call | flops 10000000000 | bytes 33554432 | tf_op jit(solution)/shard_map/decode/pallas_call | solution.py:421
  54.2 0.0 copy-done.2
  54.2 0.0 copy-done.1
  54.2 0.0 copy-done
  54.2 7.2 %store.1 = (bf16[64,64,8,128]{3,2,1,0:T(8,128)(2,1)}, bf16[64,64,8,128]{3,2,1,0:T(8,128)(2,1)}, bf16[64,4096]{1,0:T(8,128)(2,1)}) custom-call(s32[64]{0:T(128)S(1)} %copy-done.2, bf16[64,64,8,128]{3,2,1,0:T(8,128)(2,1)S(1)} %copy-done, bf16[64,64,8,128]{3,2,1,0:T(8,128)(2,1)S(1)} %copy-done.1, bf16[64,8,128]{2,1,0:T(8,128)(2,1)S(1)} %get-tuple-element.9.kn_ref, ...), custom_call_target="tpu_custom_call" | custom-call | flops 100000000 | bytes 33554432 | tf_op jit(solution)/shard_map/store/pallas_call | solution.py:441
Async XLA Ops:
  0.6 53.6 %copy-start.2 = (s32[64]{0:T(128)S(1)}, s32[64]{0:T(128)}, u32[]{:S(2)}) copy-start(s32[64]{0:T(128)} %pos_hbm.1) | copy-start | bytes 772
  0.6 53.6 %copy-start.1 = (bf16[64,64,8,128]{3,2,1,0:T(8,128)(2,1)S(1)}, bf16[64,64,8,128]{3,2,1,0:T(8,128)(2,1)}, u32[]{:S(2)}) copy-start(bf16[64,64,8,128]{3,2,1,0:T(8,128)(2,1)} %v_ref.3) | copy-start | bytes 25165828
  0.7 53.6 %copy-start = (bf16[64,64,8,128]{3,2,1,0:T(8,128)(2,1)S(1)}, bf16[64,64,8,128]{3,2,1,0:T(8,128)(2,1)}, u32[]{:S(2)}) copy-start(bf16[64,64,8,128]{3,2,1,0:T(8,128)(2,1)} %k_ref.3) | copy-start | bytes 25165828
